TPU v7x, 256 devices: a whole 4x4x8 slice. The times are simulated.
256 devices in a mesh: dp: 32 (over z_hi, x, core), tensor: 8 (over z_lo, y).
Axes of the slice: x: 4, y: 4, z: 8 (z_hi: 4, z_lo: 2; z = z_hi * 2 + z_lo), core: 2. Of those that a mesh axis runs over, the one named last changes fastest.
Arguments:
- query_rows: bfloat16 [12288, 5120], P('dp', 'tensor'), may hold values from -128 to 128
- key_rows: bfloat16 [12288, 5120], P('dp', 'tensor'), may hold values from -5 to 5
- value_rows: bfloat16 [12288, 5120], P('dp', 'tensor'), may hold values from -12 to 12
- action_mask: int32 [32, 384], P('dp'), may hold values from 0 to 1, as said below
- residual: bfloat16 [12288, 5120], P('dp', 'tensor'), may hold values from -100 to 100
- out_weight: bfloat16 [5120, 5120], P(None, 'tensor'), may hold values from -0.078125 to 0.078125
- norm_gain: float32 [5120], P('tensor'), may hold values from 0.1 to 1.9
- upstream: bfloat16 [12288, 5120], P('dp', 'tensor'), may hold values from -6 to 6
- residual_grad: bfloat16 [12288, 5120], P('dp', 'tensor'), may hold values from -2 to 2
Outputs:
- layer_out: bfloat16 [12288, 5120], P('dp', 'tensor')
- grad_residual: bfloat16 [12288, 5120], P('dp', 'tensor')
- grad_query: bfloat16 [12288, 5120], P('dp', 'tensor')
- grad_key: bfloat16 [12288, 5120], P('dp', 'tensor')
- grad_value: bfloat16 [12288, 5120], P('dp', 'tensor')
- grad_out_weight: float32 [5120, 5120], P('dp', 'tensor')
- grad_gain: float32 [5120], P('tensor')
Inputs may be any that keep to these rules, and one draw needn't show every extreme that they name: `action_mask`: each row is a run of zeros followed by a run of ones; the ones number 1 to 192.
All inputs are finite; a program needn't handle non-finite values.
Results may differ from a plain program's by a relative error of at most 0.015.
Values may be sent and summed in bfloat16 or wider, within the bound.
A program may use at most 128 MiB of HBM per device.

v0:
```python
import jax
import jax.numpy as jnp
from jax import lax
from jax.sharding import PartitionSpec as P

D = 5120
HEAD_DIM = 128
LEN = 384


epsilon = 1e-05


def copy_for_each(value, axis):
    copies = jnp.broadcast_to(value, (lax.axis_size(axis), *value.shape))
    return lax.all_to_all(copies, axis, split_axis=0, concat_axis=0, tiled=True)


def taken_together(value, axis):
    return copy_for_each(value, axis).sum(axis=0)


def together(arrays, axis):
    vector, at, gathered = (jnp.concatenate([a.reshape(-1) for a in arrays]), 0, [])
    subtotal = taken_together(vector, axis)
    for a in arrays:
        gathered.append(subtotal[at : at + a.size].reshape(a.shape))
        at += a.size
    return tuple(gathered)


def visible(mask_row):
    position = jnp.arange(mask_row.shape[0])
    causal = position[None, :] <= position[:, None]
    observe = mask_row == 0
    return causal | observe[:, None] & observe[None, :]


def shards(
    query_rows,
    key_rows,
    value_rows,
    action_mask,
    residual,
    out_weight,
    norm_gain,
    upstream,
    residual_grad,
):
    seq_count = action_mask.shape[0]
    tok_rows = query_rows.shape[0]
    local_width = query_rows.shape[1]
    head_shape = (seq_count, LEN, local_width // HEAD_DIM, HEAD_DIM)
    query_heads = query_rows.reshape(head_shape)
    key_heads = key_rows.reshape(head_shape)
    value_heads = value_rows.reshape(head_shape)
    score_scale = HEAD_DIM ** (-0.5)
    allowed = jax.vmap(visible)(action_mask)
    scores = (
        jnp.einsum("sqhd,skhd->shqk", query_heads, key_heads, preferred_element_type=jnp.float32)
        * score_scale
    )
    masked = jnp.where(allowed[:, None], scores, -jnp.inf)
    row_top = jnp.max(masked, axis=-1, keepdims=True)
    weights = jnp.exp(masked - row_top)
    chances = weights / jnp.sum(weights, axis=-1, keepdims=True)
    chances_low = chances.astype(jnp.bfloat16)
    attended = jnp.einsum(
        "shqk,skhd->sqhd", chances_low, value_heads, preferred_element_type=jnp.float32
    )
    attended = attended.astype(jnp.bfloat16).reshape(tok_rows, local_width)
    projected = jnp.dot(attended, out_weight.T, preferred_element_type=jnp.float32)
    own_sum = lax.psum_scatter(projected, "tensor", scatter_dimension=1, tiled=True)
    layer_out = (own_sum + residual.astype(jnp.float32)).astype(jnp.bfloat16)
    out_float = layer_out.astype(jnp.float32)
    upstream_float = upstream.astype(jnp.float32)
    scaled = upstream_float * norm_gain[None, :]
    square_sum, inner_sum = together(
        (jnp.sum(out_float * out_float, axis=1), jnp.sum(scaled * out_float, axis=1)), "tensor"
    )
    row_rms = jnp.sqrt(square_sum / D + epsilon)[:, None]
    normed = out_float / row_rms
    row_inner = inner_sum[:, None] / (row_rms * D)
    grad_residual = (
        residual_grad.astype(jnp.float32) + (scaled - normed * row_inner) / row_rms
    ).astype(jnp.bfloat16)
    grad_gain = taken_together(jnp.sum(upstream_float * normed, axis=0), "dp")
    grad_full = lax.all_gather(grad_residual, "tensor", axis=1, tiled=True)
    grad_attended = jnp.dot(grad_full, out_weight, preferred_element_type=jnp.float32).astype(
        jnp.bfloat16
    )
    contract_rows = (((0,), (0,)), ((), ()))
    grad_out_weight = lax.psum_scatter(
        lax.dot_general(
            grad_full, attended, contract_rows, preferred_element_type=jnp.float32
        ).astype(jnp.bfloat16),
        "dp",
        scatter_dimension=0,
        tiled=True,
    ).astype(jnp.float32)
    grad_heads = grad_attended.reshape(head_shape)
    grad_value = jnp.einsum(
        "shqk,sqhd->skhd", chances_low, grad_heads, preferred_element_type=jnp.float32
    ).astype(jnp.bfloat16)
    grad_chances = jnp.einsum(
        "sqhd,skhd->shqk", grad_heads, value_heads, preferred_element_type=jnp.float32
    )
    row_delta = jnp.sum(chances * grad_chances, axis=-1, keepdims=True)
    grad_scores = (chances * (grad_chances - row_delta) * score_scale).astype(jnp.bfloat16)
    grad_query = jnp.einsum(
        "shqk,skhd->sqhd", grad_scores, key_heads, preferred_element_type=jnp.float32
    ).astype(jnp.bfloat16)
    grad_key = jnp.einsum(
        "shqk,sqhd->skhd", grad_scores, query_heads, preferred_element_type=jnp.float32
    ).astype(jnp.bfloat16)
    return (
        layer_out,
        grad_residual,
        grad_query.reshape(tok_rows, local_width),
        grad_key.reshape(tok_rows, local_width),
        grad_value.reshape(tok_rows, local_width),
        grad_out_weight,
        grad_gain,
    )


def solution(mesh):
    placed = (
        P("dp", "tensor"),
        P("dp", "tensor"),
        P("dp", "tensor"),
        P("dp", None),
        P("dp", "tensor"),
        P(None, "tensor"),
        P("tensor"),
        P("dp", "tensor"),
        P("dp", "tensor"),
    )
    return jax.shard_map(
        shards,
        mesh=mesh,
        in_specs=placed,
        out_specs=(
            P("dp", "tensor"),
            P("dp", "tensor"),
            P("dp", "tensor"),
            P("dp", "tensor"),
            P("dp", "tensor"),
            P("dp", "tensor"),
            P("tensor"),
        ),
        check_vma=False,
    )
```

profile of v0, /device:TPU:56, one launch (start us, length us, event | category | flops | bytes accessed | tf_op | source)
XLA Modules:
  0.0 307.6 jit_solution(5571420122219654307)
XLA Ops:
  7.2 1.3 copy.65
  9.4 1.3 copy.61
  10.7 2.2 copy.62
  12.9 4.0 %fusion.41 = (f32[5,384]{1,0:T(8,128)S(1)}, f32[5,384,384]{1,2,0:T(8,128)}) fusion(pred[384,384]{0,1:T(8,128)(4,1)S(1)} %fusion.32, bf16[384,5,128]{0,2,1:T(8,128)(2,1)S(1)} %bitcast.54, bf16[384,5,128]{0,2,1:T(8,128)(2,1)} %bitcast.56), kind=kOutput, calls=%fused_computation.50 | convolution fusion | flops 191693184 | bytes 4087296 | tf_op jit(solution)/shard_map/sub | solution.py:65
  16.9 2.5 convolution_convert_fusion.2
  20.2 5.4 %fusion.42 = f32[384,5120]{1,0:T(8,128)} fusion(bf16[384,640]{0,1:T(8,128)(2,1)S(1)} %bitcast.52, bf16[5120,640]{1,0:T(8,128)(2,1)S(1)} %bitcast.47), kind=kOutput, calls=%fused_computation.51 | convolution fusion | flops 2516582400 | bytes 14909440 | tf_op jit(solution)/shard_map/dot_general | solution.py:72
  25.6 89.9 %reduce-scatter.3.cloned.1.call-done = f32[384,640]{1,0:T(8,128)} async-done(((f32[384,5120]{1,0:T(8,128)}), f32[384,640]{1,0:T(8,128)}) %reduce-scatter.3.cloned.1.call-update) | async-done | bytes 983056 | tf_op jit(solution)/shard_map/reduce_scatter | solution.py:73
  115.6 1.6 fusion.27
  117.2 9.2 %all_to_all.12 = f32[8,1,768]{2,1,0:T(1,128)S(1)} all-to-all(f32[8,1,768]{2,1,0:T(1,128)S(1)} %broadcast_in_dim.18), channel_id=1, replica_groups=mesh['dp'=32,'tensor'=8] {'tensor'}, dimensions={0} | all-to-all | bytes 49152 | tf_op jit(solution)/shard_map/all_to_all | solution.py:16
  126.4 1.3 fusion.26
  127.8 51.9 %all-gather.2.cloned.1.call-done = bf16[384,5120]{1,0:T(8,128)(2,1)} async-done(((bf16[384,640]{1,0:T(8,128)(2,1)}), bf16[384,5120]{1,0:T(8,128)(2,1)}) %all-gather.2.cloned.1.call-update) | async-done | bytes 3932176 | tf_op jit(solution)/shard_map/all_gather | solution.py:88
  179.7 8.8 %convolution_convert_fusion = bf16[5120,640]{1,0:T(8,128)(2,1)} fusion(bf16[384,5120]{1,0:T(8,128)(2,1)} %all-gather.2.cloned.1.call-done, bf16[384,640]{0,1:T(8,128)(2,1)S(1)} %bitcast.53), kind=kOutput, calls=%fused_computation.2 | convolution fusion | flops 2519859200 | bytes 10977280 | tf_op jit(solution)/shard_map/dot_general | solution.py:94
  188.6 19.0 %all_to_all.13 = f32[32,1,640]{2,1,0:T(1,128)S(1)} all-to-all(f32[32,1,640]{2,1,0:T(1,128)S(1)} %broadcast_in_dim.19), channel_id=1, replica_groups=mesh['dp'=32,'tensor'=8] {'dp'}, dimensions={0} | all-to-all | bytes 163840 | tf_op jit(solution)/shard_map/all_to_all | solution.py:16
  208.3 7.7 %convolution_convert_fusion.1 = bf16[384,640]{1,0:T(8,128)(2,1)S(1)} fusion(bf16[384,5120]{1,0:T(8,128)(2,1)} %all-gather.2.cloned.1.call-done, bf16[5120,640]{1,0:T(8,128)(2,1)} %param.14), kind=kOutput, calls=%fused_computation.20 | convolution fusion | flops 2516828160 | bytes 10977280 | tf_op jit(solution)/shard_map/dot_general | solution.py:89
  216.0 1.0 copy.68
  217.1 1.7 fusion.43
  218.7 4.2 %fusion.17 = bf16[5,384,128]{1,2,0:T(8,128)(2,1)S(1)} fusion(bf16[384,5,128]{0,2,1:T(8,128)(2,1)} %bitcast.57, f32[5,384,384]{1,2,0:T(8,128)S(1)} %fusion.43, f32[5,384,384]{1,2,0:T(8,128)} %get-tuple-element.43, f32[5,384]{1,0:T(8,128)S(1)} %get-tuple-element.42), kind=kOutput, calls=%fused_computation.21 | convolution fusion | flops 194152704 | bytes 6888960 | tf_op jit(solution)/shard_map/shqk,skhd->sqhd/dot_general | solution.py:110
  222.9 1.0 copy.75
  223.9 4.8 %fusion.20 = bf16[5,384,128]{1,2,0:T(8,128)(2,1)} fusion(bf16[384,5,128]{0,2,1:T(8,128)(2,1)} %bitcast.55, f32[5,384,384]{1,2,0:T(8,128)S(1)} %fusion.43, f32[5,384,384]{1,2,0:T(8,128)} %get-tuple-element.43, f32[5,384]{1,0:T(8,128)S(1)} %get-tuple-element.42), kind=kOutput, calls=%fused_computation.22 | convolution fusion | flops 194152704 | bytes 6888960 | tf_op jit(solution)/shard_map/shqk,sqhd->skhd/dot_general | solution.py:113
  228.7 2.0 copy.76
  230.8 2.4 convolution_convert_fusion.3
  233.2 1.0 copy.77
  234.2 65.2 %reduce-scatter.5.cloned.1.call-done = bf16[160,640]{1,0:T(8,128)(2,1)} async-done(((bf16[5120,640]{1,0:T(8,128)(2,1)}), bf16[160,640]{1,0:T(8,128)(2,1)}) %reduce-scatter.5.cloned.1.call-update) | async-done | bytes 204816 | tf_op jit(solution)/shard_map/reduce_scatter | solution.py:93
  299.4 1.7 convert_element_type.105
  (41 shorter events, 2.6 us)
Async XLA Ops:
  7.2 108.4 %reduce-scatter.3.cloned.1.call-start = ((), (), s32[]{:S(2)}) async-start(), calls=%async_computation.4 | async-start | bytes 8847360 | tf_op jit(solution)/shard_map/reduce_scatter | solution.py:73
  8.5 8.4 %copy-start.2 = (bf16[384,640]{0,1:T(8,128)(2,1)}, bf16[384,640]{0,1:T(8,128)(2,1)S(1)}, u32[]{:S(2)}) copy-start(bf16[384,640]{0,1:T(8,128)(2,1)S(1)} %copy.65) | copy-start | bytes 1474564
  10.7 8.7 %copy-start.8 = (bf16[384,640]{0,1:T(8,128)(2,1)}, bf16[384,640]{0,1:T(8,128)(2,1)S(1)}, u32[]{:S(2)}) copy-start(bf16[384,640]{0,1:T(8,128)(2,1)S(1)} %copy.61) | copy-start | bytes 1474564
  12.9 7.3 %slice-start = ((s8[6553600]{0:T(1024)(128)(4,1)}), s8[2359296]{0:T(1024)(128)(4,1)S(1)}, s32[]{:S(2)}) async-start(s8[6553600]{0:T(1024)(128)(4,1)} %bitcast.46), calls=%async_computation.7 | async-start | bytes 4718592
  16.9 3.3 %slice-start.1 = ((s8[6553600]{0:T(1024)(128)(4,1)}), s8[4194304]{0:T(1024)(128)(4,1)S(1)}, s32[]{:S(2)}) async-start(s8[6553600]{0:T(1024)(128)(4,1)} %bitcast.46), calls=%async_computation.8 | async-start | bytes 8388608
  19.4 0.8 copy-start.5
  25.5 90.0 %copy-start = (bf16[384,640]{1,0:T(8,128)(2,1)S(1)}, bf16[384,640]{1,0:T(8,128)(2,1)}, u32[]{:S(2)}) copy-start(bf16[384,640]{1,0:T(8,128)(2,1)} %param.16) | copy-start | bytes 1474564
  25.6 90.0 %copy-start.7 = (bf16[384,640]{1,0:T(8,128)(2,1)S(1)}, bf16[384,640]{1,0:T(8,128)(2,1)}, u32[]{:S(2)}) copy-start(bf16[384,640]{1,0:T(8,128)(2,1)} %param.13) | copy-start | bytes 1474564
  25.6 90.0 %copy-start.10 = (f32[640]{0:T(1024)S(1)}, f32[640]{0:T(1024)}, u32[]{:S(2)}) copy-start(f32[640]{0:T(1024)} %param.15) | copy-start | bytes 7684
  25.6 100.9 %copy-start.9 = (bf16[384,640]{1,0:T(8,128)(2,1)S(1)}, bf16[384,640]{1,0:T(8,128)(2,1)}, u32[]{:S(2)}) copy-start(bf16[384,640]{1,0:T(8,128)(2,1)} %param.17) | copy-start | bytes 1474564
  25.6 154.2 %copy-start.6 = (bf16[5,384,128]{1,2,0:T(8,128)(2,1)S(1)}, bf16[5,384,128]{1,2,0:T(8,128)(2,1)}, u32[]{:S(2)}) copy-start(bf16[5,384,128]{1,2,0:T(8,128)(2,1)} %copy-done.5) | copy-start | bytes 1474564
  25.6 154.1 %all-gather.2.cloned.1.call-start = ((), (), s32[]{:S(2)}) async-start(), calls=%async_computation.5 | async-start | bytes 4423680 | tf_op jit(solution)/shard_map/all_gather | solution.py:88
  117.2 71.4 %copy-start.1 = (bf16[384,640]{1,0:T(8,128)(2,1)}, bf16[384,640]{1,0:T(8,128)(2,1)S(1)}, u32[]{:S(2)}) copy-start(bf16[384,640]{1,0:T(8,128)(2,1)S(1)} %get-tuple-element.37) | copy-start | bytes 1474564
  127.7 171.7 %reduce-scatter.5.cloned.1.call-start = ((), (), s32[]{:S(2)}) async-start(), calls=%async_computation.6 | async-start | bytes 6758400 | tf_op jit(solution)/shard_map/reduce_scatter | solution.py:93
  208.3 8.7 %copy-start.3 = (bf16[384,640]{0,1:T(8,128)(2,1)S(1)}, bf16[384,640]{0,1:T(8,128)(2,1)}, u32[]{:S(2)}) copy-start(bf16[384,640]{0,1:T(8,128)(2,1)} %copy-done.2) | copy-start | bytes 1474564
  223.9 6.9 %copy-start.4 = (bf16[384,640]{0,1:T(8,128)(2,1)S(1)}, bf16[384,640]{0,1:T(8,128)(2,1)}, u32[]{:S(2)}) copy-start(bf16[384,640]{0,1:T(8,128)(2,1)} %copy.68) | copy-start | bytes 1474564
Sparse Core Ops, SparseCore 0:
  25.7 89.8 reduce-scatter.2
  127.9 51.8 all-gather.1
  188.7 110.6 reduce-scatter.4
where the time goes:
time: 310 us; the launch traced here: 308 us
  waiting for transfers between devices  207 us (67%)
  matrix products  41.5 us (13%)
  blocking collectives  28.2 us (9%)
  between operations  13.9 us (4%)
  local copies, waits for them, and re-layouts  10.7 us (3%)
  other arithmetic  6.13 us (2%)
    reduce_scatter x1, waiting for transfers between devices, shards(): lax.psum_scatter(projected, 'tensor', scatter_dimension=1, tiled=True)  89.9 us
    reduce_scatter x1, waiting for transfers between devices, shards(): lax.psum_scatter(lax.dot_general(grad_full, attended, contract_rows, pref...  65.2 us
    all_gather x1, waiting for transfers between devices, shards(): grad_full = lax.all_gather(grad_residual, 'tensor', axis=1, tiled=True)  51.9 us
    all_to_all x2, blocking collectives, copy_for_each(): return lax.all_to_all(copies, axis, split_axis=0, concat_axis=0, tiled=True)  28.2 us
    unnamed x32, local copies, waits for them, and re-layouts  9.62 us
    dot_general x1, matrix products, shards(): lax.dot_general(grad_full, attended, contract_rows, preferred_element_typ...  8.83 us
    dot_general x1, matrix products, shards(): jnp.dot(grad_full, out_weight, preferred_element_type=jnp.float32)  7.72 us
  transfers between devices with their start and end apart: 3, of which 3 were waited for; matrix products, arithmetic and copies ran while one was open for 9% of the time, Pallas kernels for 0%

commit v1 on v0

v1 whole, which is shorter than its diff:
```python
import functools

import jax
import jax.numpy as jnp
from jax import lax
from jax.experimental import pallas as pl
from jax.experimental.pallas import tpu as pltpu
from jax.sharding import PartitionSpec as P

MESH = pl.DeviceIdType.MESH
F32 = jnp.float32
BF16 = jnp.bfloat16

D = 5120
HEAD_DIM = 128
LEN = 384
WIDTH = 640
HEADS = WIDTH // HEAD_DIM
CA = 256
CB = WIDTH - CA
HALF = LEN // 2
OUT_ROWS = 160
HALF_ROWS = OUT_ROWS // 2
SCALE = HEAD_DIM ** (-0.5)
EPSILON = 1e-05
MESSAGES = 128


def dot(a, b, ca, cb):
    return lax.dot_general(a, b, (((ca,), (cb,)), ((), ())), preferred_element_type=F32)


def kernel(
    q_hbm, k_hbm, v_hbm, mask_ref, res_hbm, w_hbm, gain_ref, ups_hbm, rg_hbm,
    lo_hbm, gr_hbm, gq_hbm, gk_hbm, gv_hbm, gw_hbm, gg_ref,
    q, k, v, res, w, ups, rg, bias, probs, att, lo, gr, ga, gacc, gq, gk, gv, gw_out,
    pa, pb, rec_az, rec_a, rec_b, mer_a, mer_b, zb_send, zb_rec, own,
    stat, stat_rec, all_a, all_b,
    gwb, cx_rec, u, x_rec, x_mer, z_send, z_rec, z_own,
    gain0, gain0_rec, gain1, gain1_rec, gain2, gain2_rec,
    ssem, rsem, lsem,
):
    t = lax.axis_index("tensor")
    dp = lax.axis_index("dp")
    z, y = t // 4, t % 4
    c, x, zh = dp % 2, (dp // 2) % 4, dp // 8

    def at_y(step):
        return {"tensor": z * 4 + (y + step) % 4}

    z_peer = {"tensor": (1 - z) * 4 + y}
    c_peer = {"dp": dp + 1 - 2 * c}

    def at_x(step):
        return {"dp": zh * 8 + ((x + step) % 4) * 2 + c}

    def at_zh(step):
        return {"dp": ((zh + step) % 4) * 8 + x * 2 + c}

    peers = [{"tensor": (t + j) % 8} for j in range(1, 8)]
    peers += [c_peer]
    peers += [at_x(s) for s in (1, 2, 3)]
    peers += [at_zh(s) for s in (1, 2, 3)]

    local = []

    def fetch(src, dst):
        copy = pltpu.make_async_copy(src, dst, lsem.at[len(local)])
        local.append(copy)
        copy.start()
        return copy

    in_q, in_k, in_v = fetch(q_hbm, q), fetch(k_hbm, k), fetch(v_hbm, v)
    in_w = fetch(w_hbm, w)
    in_res, in_ups, in_rg = fetch(res_hbm, res), fetch(ups_hbm, ups), fetch(rg_hbm, rg)

    barrier = pltpu.get_barrier_semaphore()
    for peer in peers:
        pl.semaphore_signal(barrier, inc=1, device_id=peer, device_id_type=MESH)

    messages = []

    def message(src, dst, device, start=True):
        i = len(messages)
        copy = pltpu.make_async_remote_copy(
            src_ref=src, dst_ref=dst, send_sem=ssem.at[i], recv_sem=rsem.at[i],
            device_id=device, device_id_type=MESH,
        )
        messages.append(copy)
        if start:
            copy.start()
        return copy

    zeros = jnp.sum(1 - mask_ref[...], axis=1, keepdims=True)
    row = lax.broadcasted_iota(jnp.int32, (LEN, LEN), 0)
    col = lax.broadcasted_iota(jnp.int32, (LEN, LEN), 1)
    allowed = (col <= row) | (jnp.maximum(row, col) < zeros)
    bias[...] = jnp.where(allowed, 0.0, -jnp.inf).astype(F32)
    in_q.wait()
    in_k.wait()
    in_v.wait()

    def head_cols(h):
        return pl.ds(pl.multiple_of(h * HEAD_DIM, HEAD_DIM), HEAD_DIM)

    def forward(h, carry):
        cols = head_cols(h)
        s = dot(q[:, cols], k[:, cols], 1, 1) * SCALE + bias[...]
        e = jnp.exp(s - jnp.max(s, axis=1, keepdims=True))
        p = e * (1.0 / jnp.sum(e, axis=1, keepdims=True))
        probs[h] = p
        att[:, cols] = dot(p.astype(BF16), v[:, cols], 1, 0).astype(BF16)
        return carry

    lax.fori_loop(0, HEADS, forward, 0)
    in_w.wait()

    def w_rows(block):
        return pl.ds(pl.multiple_of(block * WIDTH, WIDTH), WIDTH)

    def project(d):
        def one(j, carry):
            zz = j * z + (1 - j) * (1 - z)
            block = zz * 4 + (y + d) % 4
            r = dot(att[...], w[w_rows(block), :], 1, 1)
            pa[d, j] = r[:, :CA].astype(BF16)
            pb[d, zz] = r[:, CA:].astype(BF16)
            return carry

        lax.fori_loop(0, 2, one, 0)

    first, second = pl.ds(0, HALF), pl.ds(HALF, HALF)
    az, b1, b2, a1, a2 = {}, {}, {}, {}, {}
    project(2)
    pl.semaphore_wait(barrier, len(peers))
    b1[1] = message(pb.at[2, :, first], rec_b.at[0], at_y(1))
    b1[-1] = message(pb.at[2, :, second], rec_b.at[1], at_y(-1))
    az[2] = message(pa.at[2, 0], rec_az.at[2], z_peer)
    project(1)
    b2[1] = message(pb.at[1, :, second], rec_b.at[2], at_y(1))
    az[1] = message(pa.at[1, 0], rec_az.at[1], z_peer)
    project(3)
    b2[-1] = message(pb.at[3, :, first], rec_b.at[3], at_y(-1))
    az[3] = message(pa.at[3, 0], rec_az.at[3], z_peer)
    project(0)
    az[0] = message(pa.at[0, 0], rec_az.at[0], z_peer)

    b1[1].wait_recv()
    mer_b[0] = pb[1, :, :HALF] + rec_b[0]
    b3 = {1: message(mer_b.at[0], rec_b.at[4], at_y(1))}
    b1[-1].wait_recv()
    mer_b[1] = pb[3, :, HALF:] + rec_b[1]
    b3[-1] = message(mer_b.at[1], rec_b.at[5], at_y(-1))

    def join(d):
        az[d].wait_recv()
        pa[d, 1] = pa[d, 1] + rec_az[d]

    join(2)
    a1[1] = message(pa.at[2, 1, first], rec_a.at[0], at_y(1))
    a1[-1] = message(pa.at[2, 1, second], rec_a.at[1], at_y(-1))
    join(1)
    a2[1] = message(pa.at[1, 1, second], rec_a.at[2], at_y(1))
    join(3)
    a2[-1] = message(pa.at[3, 1, first], rec_a.at[3], at_y(-1))
    az[0].wait_recv()

    b2[1].wait_recv()
    b2[-1].wait_recv()
    b3[1].wait_recv()
    b3[-1].wait_recv()

    def b_sum(zz):
        top = pb[0, zz, :HALF].astype(F32) + rec_b[3, zz].astype(F32) + rec_b[4, zz].astype(F32)
        low = pb[0, zz, HALF:].astype(F32) + rec_b[2, zz].astype(F32) + rec_b[5, zz].astype(F32)
        return top, low

    top, low = b_sum(1 - z)
    zb_send[:HALF] = top.astype(BF16)
    zb_send[HALF:] = low.astype(BF16)
    zb = message(zb_send, zb_rec, z_peer)

    a1[1].wait_recv()
    mer_a[0] = pa[1, 1, :HALF] + rec_a[0]
    a3 = {1: message(mer_a.at[0], rec_a.at[4], at_y(1))}
    a1[-1].wait_recv()
    mer_a[1] = pa[3, 1, HALF:] + rec_a[1]
    a3[-1] = message(mer_a.at[1], rec_a.at[5], at_y(-1))

    in_res.wait()
    in_ups.wait()
    in_rg.wait()
    top, low = b_sum(z)
    own[:HALF, CA:] = top
    own[HALF:, CA:] = low
    own[:, :CA] = pa[0, 1].astype(F32) + rec_az[0].astype(F32)

    zb.wait_recv()
    own_b = own[:, CA:] + zb_rec[...].astype(F32) + res[:, CA:].astype(F32)
    low_b = own_b.astype(BF16)
    lo[:, CA:] = low_b
    f_b = low_b.astype(F32)
    scaled_b = ups[:, CA:].astype(F32) * gain_ref[:, CA:]
    square = jnp.sum(f_b * f_b, axis=1, keepdims=True)
    inner = jnp.sum(f_b * scaled_b, axis=1, keepdims=True)

    a2[1].wait_recv()
    a2[-1].wait_recv()
    a3[1].wait_recv()
    a3[-1].wait_recv()
    top = own[:HALF, :CA] + rec_a[3].astype(F32) + rec_a[4].astype(F32) + res[:HALF, :CA].astype(F32)
    low = own[HALF:, :CA] + rec_a[2].astype(F32) + rec_a[5].astype(F32) + res[HALF:, :CA].astype(F32)
    lo[:HALF, :CA] = top.astype(BF16)
    lo[HALF:, :CA] = low.astype(BF16)
    f_a = lo[:, :CA].astype(F32)
    scaled_a = ups[:, :CA].astype(F32) * gain_ref[:, :CA]
    square = square + jnp.sum(f_a * f_a, axis=1, keepdims=True)
    inner = inner + jnp.sum(f_a * scaled_a, axis=1, keepdims=True)

    lane = lax.broadcasted_iota(jnp.int32, (LEN, 128), 1)
    packed = jnp.where(lane == 0, square, jnp.where(lane == 1, inner, 0.0))
    stat[...] = packed.T[:8]
    stats = [message(stat, stat_rec.at[j], peers[j - 1]) for j in range(1, 8)]
    out_lo = fetch(lo, lo_hbm)
    total = stat[...]
    for j in range(1, 8):
        stats[j - 1].wait_recv()
        total = total + stat_rec[j]
    wide = jnp.concatenate([total, jnp.zeros((120, LEN), F32)], axis=0).T
    square, inner = wide[:, 0:1], wide[:, 1:2]
    rms = jnp.sqrt(square / D + EPSILON)
    back = 1.0 / rms
    row_inner = inner / (rms * D)

    def grad_rows(lo_part, ups_part, gain_part, rg_part):
        up = ups_part.astype(F32)
        normed = lo_part.astype(F32) * back
        g = rg_part.astype(F32) + (up * gain_part - normed * row_inner) * back
        return g.astype(BF16), (up * normed).reshape(LEN // 8, 8, -1).sum(axis=0)

    g, gain_a = grad_rows(lo[:, :CA], ups[:, :CA], gain_ref[:, :CA], rg[:, :CA])
    all_a[t] = g
    gr[:, :CA] = g
    mine_a = all_a.at[t]
    first_a = all_a.at[t, first]
    second_a = all_a.at[t, second]
    y1 = {}
    y1["a", 1, 1] = message(first_a, first_a, at_y(1))
    y1["a", -1, 1] = message(second_a, second_a, at_y(-1))
    g, gain_b = grad_rows(lo[:, CA:], ups[:, CA:], gain_ref[:, CA:], rg[:, CA:])
    all_b[t] = g
    gr[:, CA:] = g
    zx_b = message(all_b.at[t], all_b.at[t], z_peer)
    zx_a = {0: message(mine_a, mine_a, z_peer)}
    first_b = all_b.at[t, first]
    second_b = all_b.at[t, second]
    y1["b", 1, 1] = message(first_b, first_b, at_y(1))
    y1["b", -1, 1] = message(second_b, second_b, at_y(-1))
    y1["a", 1, 2] = message(second_a, second_a, at_y(1))
    y1["a", -1, 2] = message(first_a, first_a, at_y(-1))
    y1["b", 1, 2] = message(second_b, second_b, at_y(1))
    y1["b", -1, 2] = message(first_b, first_b, at_y(-1))
    gain0[:, :CA] = gain_a
    gain0[:, CA:] = gain_b
    gain_c = message(gain0, gain0_rec, c_peer)
    out_gr = fetch(gr, gr_hbm)

    def block_at(zz, step):
        return zz * 4 + (y + step) % 4

    def forward_on(buf, zz, sent, key):
        sent[key, 1, 1].wait_recv()
        part = buf.at[block_at(zz, -1), first]
        sent[key, 1, 3] = message(part, part, at_y(1))
        sent[key, -1, 1].wait_recv()
        part = buf.at[block_at(zz, 1), second]
        sent[key, -1, 3] = message(part, part, at_y(-1))

    def across(step):
        part = all_a.at[block_at(z, step)]
        zx_a[step] = message(part, part, z_peer)

    def accumulate(blocks, start):
        def one(j, carry):
            block = blocks(j)
            grad = jnp.concatenate([all_a[block], all_b[block]], axis=1)
            r = dot(grad, w[w_rows(block), :], 1, 0)
            if start:
                gacc[...] = r
            else:
                gacc[...] += r
            return carry

        lax.fori_loop(0, 1 if start else 2, one, 0)

    def group_of(g):
        zz = z if g < 2 else 1 - z
        pair = y // 2 if g % 2 == 0 else 1 - y // 2
        return zz * 2 + pair

    cx = {}

    def weight_grad(g):
        kk = group_of(g)

        def one(j, carry):
            block = kk * 2 + j
            grad = jnp.concatenate([all_a[block], all_b[block]], axis=1)
            r = dot(grad, att[...], 0, 0).astype(BF16)
            for s in range(4):
                gwb[g, s % 2, 2 * j + s // 2] = r[s * OUT_ROWS : (s + 1) * OUT_ROWS]
            return carry

        lax.fori_loop(0, 2, one, 0)
        cx[g] = message(gwb.at[g, 1 - c], cx_rec.at[g], c_peer)

    low_rows, high_rows = pl.ds(0, HALF_ROWS), pl.ds(HALF_ROWS, HALF_ROWS)
    xs = {}

    def x_first(g):
        cx[g].wait_recv()

        def u_of(d):
            to = (x + d) % 4
            u[g, d] = gwb[g, c, to] + cx_rec[g, to]

        u_of(2)
        xs[g, 1, 1] = message(u.at[g, 2, low_rows], x_rec.at[g, 0], at_x(1))
        xs[g, -1, 1] = message(u.at[g, 2, high_rows], x_rec.at[g, 1], at_x(-1))
        u_of(1)
        xs[g, 1, 2] = message(u.at[g, 1, high_rows], x_rec.at[g, 2], at_x(1))
        u_of(3)
        xs[g, -1, 2] = message(u.at[g, 3, low_rows], x_rec.at[g, 3], at_x(-1))
        u_of(0)

    def x_second(g):
        xs[g, 1, 1].wait_recv()
        x_mer[g, 0] = u[g, 1, :HALF_ROWS] + x_rec[g, 0]
        xs[g, 1, 3] = message(x_mer.at[g, 0], x_rec.at[g, 4], at_x(1))
        xs[g, -1, 1].wait_recv()
        x_mer[g, 1] = u[g, 3, HALF_ROWS:] + x_rec[g, 1]
        xs[g, -1, 3] = message(x_mer.at[g, 1], x_rec.at[g, 5], at_x(-1))

    zs = {}

    def z_copy(g):
        kk = group_of(g)
        d = (kk - zh) % 4
        slot = (d + 3) % 4
        return d, pltpu.make_async_remote_copy(
            src_ref=z_send.at[g], dst_ref=z_rec.at[slot],
            send_sem=ssem.at[MESSAGES - 4 + g], recv_sem=rsem.at[MESSAGES - 4 + slot],
            device_id={"dp": kk * 8 + x * 2 + c}, device_id_type=MESH,
        )

    def x_last(g):
        for step in (1, -1):
            xs[g, step, 2].wait_recv()
            xs[g, step, 3].wait_recv()
        upper = u[g, 0, :HALF_ROWS].astype(F32) + x_rec[g, 3].astype(F32) + x_rec[g, 4].astype(F32)
        lower = u[g, 0, HALF_ROWS:].astype(F32) + x_rec[g, 2].astype(F32) + x_rec[g, 5].astype(F32)
        z_send[g, :HALF_ROWS] = upper.astype(BF16)
        z_send[g, HALF_ROWS:] = lower.astype(BF16)
        d, copy = z_copy(g)

        @pl.when(d != 0)
        def _():
            copy.start()

        @pl.when(d == 0)
        def _():
            z_own[:HALF_ROWS] = upper
            z_own[HALF_ROWS:] = lower

    accumulate(lambda j: t, True)
    forward_on(all_a, z, y1, "a")
    forward_on(all_b, z, y1, "b")
    zx_b.wait_recv()
    y2 = {}
    other = block_at(1 - z, 0)
    first_p = all_b.at[other, first]
    second_p = all_b.at[other, second]
    y2["b", 1, 1] = message(first_p, first_p, at_y(1))
    y2["b", -1, 1] = message(second_p, second_p, at_y(-1))
    y2["b", 1, 2] = message(second_p, second_p, at_y(1))
    y2["b", -1, 2] = message(first_p, first_p, at_y(-1))
    y1["a", 1, 2].wait_recv()
    across(-1)
    y1["a", -1, 2].wait_recv()
    across(1)
    gain_c.wait_recv()
    gain1[...] = gain0[...] + gain0_rec[...]
    gain_x = [message(gain1, gain1_rec.at[s - 1], at_x(s)) for s in (1, 2, 3)]
    y1["b", 1, 2].wait_recv()
    y1["b", -1, 2].wait_recv()
    weight_grad(0)
    x_first(0)
    y1["a", 1, 3].wait_recv()
    y1["a", -1, 3].wait_recv()
    across(2)
    accumulate(lambda j: block_at(z, 1) * j + block_at(z, -1) * (1 - j), False)
    x_second(0)
    y1["b", 1, 3].wait_recv()
    y1["b", -1, 3].wait_recv()
    weight_grad(1)
    x_first(1)
    x_second(1)
    forward_on(all_b, 1 - z, y2, "b")
    zx_a[0].wait_recv()
    accumulate(lambda j: block_at(z, 2) * j + block_at(1 - z, 0) * (1 - j), False)
    for copy in gain_x:
        copy.wait_recv()
    gain2[...] = gain1[...] + gain1_rec[0] + gain1_rec[1] + gain1_rec[2]
    gain_z = [message(gain2, gain2_rec.at[s - 1], at_zh(s)) for s in (1, 2, 3)]
    x_last(0)
    zx_a[-1].wait_recv()
    zx_a[1].wait_recv()
    y2["b", 1, 2].wait_recv()
    y2["b", -1, 2].wait_recv()
    weight_grad(2)
    x_first(2)
    accumulate(lambda j: block_at(1 - z, 1) * j + block_at(1 - z, -1) * (1 - j), False)
    zx_a[2].wait_recv()
    y2["b", 1, 3].wait_recv()
    y2["b", -1, 3].wait_recv()
    weight_grad(3)
    x_first(3)
    x_second(2)
    last = block_at(1 - z, 2)
    grad = jnp.concatenate([all_a[last], all_b[last]], axis=1)
    ga[...] = (gacc[...] + dot(grad, w[w_rows(last), :], 1, 0)).astype(BF16)
    x_last(1)

    def backward(h, carry):
        cols = head_cols(h)
        g_head = ga[:, cols]
        p = probs[h]
        gv[:, cols] = dot(p.astype(BF16), g_head, 0, 0).astype(BF16)
        gp = dot(g_head, v[:, cols], 1, 1)
        delta = jnp.sum(p * gp, axis=1, keepdims=True)
        gs = (p * (gp - delta) * SCALE).astype(BF16)
        gq[:, cols] = dot(gs, k[:, cols], 1, 0).astype(BF16)
        gk[:, cols] = dot(gs, q[:, cols], 0, 0).astype(BF16)
        return carry

    lax.fori_loop(0, 2, backward, 0)
    x_second(3)
    lax.fori_loop(2, 4, backward, 0)
    x_last(2)
    lax.fori_loop(4, HEADS, backward, 0)
    out_gq, out_gk, out_gv = fetch(gq, gq_hbm), fetch(gk, gk_hbm), fetch(gv, gv_hbm)
    for copy in gain_z:
        copy.wait_recv()
    gain = gain2[...] + gain2_rec[0] + gain2_rec[1] + gain2_rec[2]
    gg_ref[...] = jnp.sum(gain, axis=0, keepdims=True)
    x_last(3)

    for slot in range(3):
        pltpu.make_async_remote_copy(
            src_ref=z_send.at[0], dst_ref=z_rec.at[slot],
            send_sem=ssem.at[MESSAGES - 4], recv_sem=rsem.at[MESSAGES - 4 + slot],
            device_id=c_peer, device_id_type=MESH,
        ).wait_recv()
    gw_out[...] = (
        z_own[...] + z_rec[0].astype(F32) + z_rec[1].astype(F32) + z_rec[2].astype(F32)
    )
    out_gw = fetch(gw_out, gw_hbm)

    for copy in messages:
        copy.wait_send()
    for g in range(4):
        d, copy = z_copy(g)

        @pl.when(d != 0)
        def _():
            copy.wait_send()

    for copy in (out_lo, out_gr, out_gq, out_gk, out_gv, out_gw):
        copy.wait()
    assert len(messages) <= MESSAGES - 4


def shards(q, k, v, mask, res, w, gain, ups, rg):
    rows = jax.ShapeDtypeStruct((LEN, WIDTH), BF16)
    anywhere = pl.BlockSpec(memory_space=pl.ANY)
    vmem = pl.BlockSpec(memory_space=pltpu.VMEM)

    def b(*shape):
        return pltpu.VMEM(shape, BF16)

    def f(*shape):
        return pltpu.VMEM(shape, F32)

    slab = (LEN, WIDTH)
    part = (OUT_ROWS, WIDTH)
    half = (HALF_ROWS, WIDTH)
    scratch = [
        b(*slab), b(*slab), b(*slab), b(*slab), b(D, WIDTH), b(*slab), b(*slab),
        f(LEN, LEN), f(HEADS, LEN, LEN), b(*slab), b(*slab), b(*slab), b(*slab), f(*slab),
        b(*slab), b(*slab), b(*slab), f(*part),
        b(4, 2, LEN, CA), b(4, 2, LEN, CB), b(4, LEN, CA), b(6, HALF, CA), b(6, 2, HALF, CB),
        b(2, HALF, CA), b(2, 2, HALF, CB), b(LEN, CB), b(LEN, CB), f(*slab),
        f(8, LEN), f(8, 8, LEN), b(8, LEN, CA), b(8, LEN, CB),
        b(4, 2, 4, *part), b(4, 4, *part), b(4, 4, *part), b(4, 6, *half), b(4, 2, *half),
        b(4, *part), b(4, *part), f(*part),
        f(8, WIDTH), f(8, WIDTH), f(8, WIDTH), f(3, 8, WIDTH), f(8, WIDTH), f(3, 8, WIDTH),
        pltpu.SemaphoreType.DMA((MESSAGES,)),
        pltpu.SemaphoreType.DMA((MESSAGES,)),
        pltpu.SemaphoreType.DMA((16,)),
    ]
    outs = pl.pallas_call(
        kernel,
        out_shape=(
            rows, rows, rows, rows, rows,
            jax.ShapeDtypeStruct(part, F32),
            jax.ShapeDtypeStruct((1, WIDTH), F32),
        ),
        in_specs=[anywhere, anywhere, anywhere, vmem, anywhere, anywhere, vmem, anywhere, anywhere],
        out_specs=(anywhere,) * 6 + (vmem,),
        scratch_shapes=scratch,
        compiler_params=pltpu.CompilerParams(
            collective_id=0, has_side_effects=True, vmem_limit_bytes=64000000
        ),
    )(q, k, v, mask, res, w, gain.reshape(1, WIDTH), ups, rg)
    return (*outs[:6], outs[6].reshape(WIDTH))


def solution(mesh):
    placed = P("dp", "tensor")
    return jax.shard_map(
        shards,
        mesh=mesh,
        in_specs=(placed, placed, placed, P("dp", None), placed, P(None, "tensor"), P("tensor"), placed, placed),
        out_specs=(placed,) * 6 + (P("tensor"),),
        check_vma=False,
    )
```

time: 310 us -> 130 us (0.42)
  waiting for transfers between devices: 207 us -> 0 us
  Pallas kernels: 0 us -> 116 us
  matrix products: 41.5 us -> 0 us
  blocking collectives: 28.2 us -> 0 us
  between operations: 13.9 us -> 0.64 us
  other arithmetic: 6.13 us -> 1.29 us
    reduce_scatter x2 -> x0, waiting for transfers between devices: 155 us -> none  [the longest x1 89.9 us: shards(): lax.psum_scatter(projected, 'tensor', scatter_dimension=1, tiled=True)]
    pallas_call x0 -> x1, Pallas kernels: none -> 116 us  [shards(): pl.pallas_call(kernel, out_shape=(rows, rows, rows, rows, rows, jax.Shape...]
    all_gather x1 -> x0, waiting for transfers between devices: 51.9 us -> none  [shards(): grad_full = lax.all_gather(grad_residual, 'tensor', axis=1, tiled=True)]
    dot_general x8 -> x0, matrix products: 37.5 us -> none  [the longest x1 8.83 us: shards(): lax.dot_general(grad_full, attended, contract_rows, preferred_element_typ...]
    all_to_all x2 -> x0, blocking collectives: 28.2 us -> none  [copy_for_each(): return lax.all_to_all(copies, axis, split_axis=0, concat_axis=0, tiled=True)]
    sub x1 -> x0, matrix products: 3.99 us -> none  [shards(): weights = jnp.exp(masked - row_top)]
    reduce_sum x4 -> x0, other arithmetic: 3.53 us -> none  [the longest x1 1.56 us: shards(): jnp.sum(out_float * out_float, axis=1)]
    unnamed x32 -> x6, local copies, waits for them, and re-layouts: 9.62 us -> 11 us
  transfers between devices with their start and end apart: 3 -> 0, of which waited for: 3 -> 0; matrix products, arithmetic and copies ran while one was open for 9% -> 0% of each run, Pallas kernels for 0% -> 0%
where the time goes in v1:
time: 130 us
  Pallas kernels  116 us (89%)
  local copies, waits for them, and re-layouts  12.3 us (9%)
    pallas_call x1, Pallas kernels, shards(): pl.pallas_call(kernel, out_shape=(rows, rows, rows, rows, rows, jax.Shape...  116 us
    unnamed x6, local copies, waits for them, and re-layouts  11 us

profile of v1, /device:TPU:56, one launch (start us, length us, event | category | flops | bytes accessed | tf_op | source)
XLA Modules:
  0.0 130.0 jit_solution(8700962125216144220)
XLA Ops:
  0.6 1.3 reshape.20.gain_ref
  1.9 115.8 %shard_map.144 = (bf16[384,640]{1,0:T(8,128)(2,1)}, bf16[384,640]{1,0:T(8,128)(2,1)}, bf16[384,640]{1,0:T(8,128)(2,1)}, bf16[384,640]{1,0:T(8,128)(2,1)}, bf16[3...) custom-call(bf16[384,640]{1,0:T(8,128)(2,1)} %q_hbm.1, bf16[384,640]{1,0:T(8,128)(2,1)} %k_hbm.1, ...), custom_call_target="tpu_custom_call" | custom-call | tf_op jit(solution)/shard_map/pallas_call | solution.py:511
  117.7 1.3 reduce
  119.0 1.8 %copy.22 = bf16[384,640]{1,0:T(8,128)(2,1)} copy(bf16[384,640]{1,0:T(8,128)(2,1)} %get-tuple-element.28) | data formatting | bytes 983040
  120.9 1.8 %copy.23 = bf16[384,640]{1,0:T(8,128)(2,1)} copy(bf16[384,640]{1,0:T(8,128)(2,1)} %get-tuple-element.29) | data formatting | bytes 983040
  122.7 1.8 %copy.24 = bf16[384,640]{1,0:T(8,128)(2,1)} copy(bf16[384,640]{1,0:T(8,128)(2,1)} %get-tuple-element.30) | data formatting | bytes 983040
  124.6 1.8 %copy.25 = bf16[384,640]{1,0:T(8,128)(2,1)} copy(bf16[384,640]{1,0:T(8,128)(2,1)} %get-tuple-element.31) | data formatting | bytes 983040
  126.4 1.8 %copy.26 = bf16[384,640]{1,0:T(8,128)(2,1)} copy(bf16[384,640]{1,0:T(8,128)(2,1)} %get-tuple-element.32) | data formatting | bytes 983040
  128.3 1.8 %copy.27 = f32[160,640]{1,0:T(8,128)} copy(f32[160,640]{1,0:T(8,128)} %get-tuple-element.33) | data formatting | bytes 819200

commit v2 on v1

--- a/solution.py
+++ b/solution.py
@@ -24,6 +24,7 @@
 SCALE = HEAD_DIM ** (-0.5)
 EPSILON = 1e-05
 MESSAGES = 128
+VMEM_LIMIT = 51 << 20
 
 
 def dot(a, b, ca, cb):
@@ -31,12 +32,12 @@
 
 
 def kernel(
-    q_hbm, k_hbm, v_hbm, mask_ref, res_hbm, w_hbm, gain_ref, ups_hbm, rg_hbm,
-    lo_hbm, gr_hbm, gq_hbm, gk_hbm, gv_hbm, gw_hbm, gg_ref,
-    q, k, v, res, w, ups, rg, bias, probs, att, lo, gr, ga, gacc, gq, gk, gv, gw_out,
+    q_hbm, k_hbm, v_hbm, mask_hbm, res_hbm, w_hbm, gain_hbm, ups_hbm, rg_hbm,
+    lo, gr, gq, gk, gv, gw_out, gg_ref,
+    q, k, v, mask_ref, res, w, gain_ref, ups, rg, bias, probs, att, ga, gacc,
     pa, pb, rec_az, rec_a, rec_b, mer_a, mer_b, zb_send, zb_rec, own,
     stat, stat_rec, all_a, all_b,
-    gwb, cx_rec, u, x_rec, x_mer, z_send, z_rec, z_own,
+    gwb, cx_rec, u, x_rec, x_mer, z_send, z_rec, z_mer, z_own,
     gain0, gain0_rec, gain1, gain1_rec, gain2, gain2_rec,
     ssem, rsem, lsem,
 ):
@@ -70,8 +71,10 @@
         copy.start()
         return copy
 
+    in_mask = fetch(mask_hbm, mask_ref)
     in_q, in_k, in_v = fetch(q_hbm, q), fetch(k_hbm, k), fetch(v_hbm, v)
     in_w = fetch(w_hbm, w)
+    in_gain = fetch(gain_hbm, gain_ref)
     in_res, in_ups, in_rg = fetch(res_hbm, res), fetch(ups_hbm, ups), fetch(rg_hbm, rg)
 
     barrier = pltpu.get_barrier_semaphore()
@@ -91,6 +94,7 @@
             copy.start()
         return copy
 
+    in_mask.wait()
     zeros = jnp.sum(1 - mask_ref[...], axis=1, keepdims=True)
     row = lax.broadcasted_iota(jnp.int32, (LEN, LEN), 0)
     col = lax.broadcasted_iota(jnp.int32, (LEN, LEN), 1)
@@ -189,6 +193,8 @@
 
     in_res.wait()
     in_ups.wait()
+    in_gain.wait()
+    gain_row = gain_ref[...].reshape(1, WIDTH)
     in_rg.wait()
     top, low = b_sum(z)
     own[:HALF, CA:] = top
@@ -200,7 +206,7 @@
     low_b = own_b.astype(BF16)
     lo[:, CA:] = low_b
     f_b = low_b.astype(F32)
-    scaled_b = ups[:, CA:].astype(F32) * gain_ref[:, CA:]
+    scaled_b = ups[:, CA:].astype(F32) * gain_row[:, CA:]
     square = jnp.sum(f_b * f_b, axis=1, keepdims=True)
     inner = jnp.sum(f_b * scaled_b, axis=1, keepdims=True)
 
@@ -213,7 +219,7 @@
     lo[:HALF, :CA] = top.astype(BF16)
     lo[HALF:, :CA] = low.astype(BF16)
     f_a = lo[:, :CA].astype(F32)
-    scaled_a = ups[:, :CA].astype(F32) * gain_ref[:, :CA]
+    scaled_a = ups[:, :CA].astype(F32) * gain_row[:, :CA]
     square = square + jnp.sum(f_a * f_a, axis=1, keepdims=True)
     inner = inner + jnp.sum(f_a * scaled_a, axis=1, keepdims=True)
 
@@ -221,7 +227,6 @@
     packed = jnp.where(lane == 0, square, jnp.where(lane == 1, inner, 0.0))
     stat[...] = packed.T[:8]
     stats = [message(stat, stat_rec.at[j], peers[j - 1]) for j in range(1, 8)]
-    out_lo = fetch(lo, lo_hbm)
     total = stat[...]
     for j in range(1, 8):
         stats[j - 1].wait_recv()
@@ -238,7 +243,7 @@
         g = rg_part.astype(F32) + (up * gain_part - normed * row_inner) * back
         return g.astype(BF16), (up * normed).reshape(LEN // 8, 8, -1).sum(axis=0)
 
-    g, gain_a = grad_rows(lo[:, :CA], ups[:, :CA], gain_ref[:, :CA], rg[:, :CA])
+    g, gain_a = grad_rows(lo[:, :CA], ups[:, :CA], gain_row[:, :CA], rg[:, :CA])
     all_a[t] = g
     gr[:, :CA] = g
     mine_a = all_a.at[t]
@@ -247,7 +252,7 @@
     y1 = {}
     y1["a", 1, 1] = message(first_a, first_a, at_y(1))
     y1["a", -1, 1] = message(second_a, second_a, at_y(-1))
-    g, gain_b = grad_rows(lo[:, CA:], ups[:, CA:], gain_ref[:, CA:], rg[:, CA:])
+    g, gain_b = grad_rows(lo[:, CA:], ups[:, CA:], gain_row[:, CA:], rg[:, CA:])
     all_b[t] = g
     gr[:, CA:] = g
     zx_b = message(all_b.at[t], all_b.at[t], z_peer)
@@ -263,7 +268,6 @@
     gain0[:, :CA] = gain_a
     gain0[:, CA:] = gain_b
     gain_c = message(gain0, gain0_rec, c_peer)
-    out_gr = fetch(gr, gr_hbm)
 
     def block_at(zz, step):
         return zz * 4 + (y + step) % 4
@@ -293,85 +297,142 @@
 
         lax.fori_loop(0, 1 if start else 2, one, 0)
 
-    def group_of(g):
-        zz = z if g < 2 else 1 - z
-        pair = y // 2 if g % 2 == 0 else 1 - y // 2
-        return zz * 2 + pair
-
+    order = [t, block_at(1 - z, 0), block_at(z, -1), block_at(z, 1), block_at(z, 2)]
+    order += [block_at(1 - z, -1), block_at(1 - z, 1), block_at(1 - z, 2)]
     cx = {}
 
-    def weight_grad(g):
-        kk = group_of(g)
-
-        def one(j, carry):
-            block = kk * 2 + j
-            grad = jnp.concatenate([all_a[block], all_b[block]], axis=1)
-            r = dot(grad, att[...], 0, 0).astype(BF16)
-            for s in range(4):
-                gwb[g, s % 2, 2 * j + s // 2] = r[s * OUT_ROWS : (s + 1) * OUT_ROWS]
-            return carry
-
-        lax.fori_loop(0, 2, one, 0)
-        cx[g] = message(gwb.at[g, 1 - c], cx_rec.at[g], c_peer)
+    def weight_grad(i):
+        grad = jnp.concatenate([all_a[order[i]], all_b[order[i]]], axis=1)
+        r = dot(grad, att[...], 0, 0).astype(BF16)
+        for s in range(4):
+            gwb[i, s % 2, s // 2] = r[s * OUT_ROWS : (s + 1) * OUT_ROWS]
+        cx[i] = message(gwb.at[i, 1 - c], cx_rec.at[i], c_peer)
 
     low_rows, high_rows = pl.ds(0, HALF_ROWS), pl.ds(HALF_ROWS, HALF_ROWS)
-    xs = {}
-
-    def x_first(g):
-        cx[g].wait_recv()
-
-        def u_of(d):
-            to = (x + d) % 4
-            u[g, d] = gwb[g, c, to] + cx_rec[g, to]
-
-        u_of(2)
-        xs[g, 1, 1] = message(u.at[g, 2, low_rows], x_rec.at[g, 0], at_x(1))
-        xs[g, -1, 1] = message(u.at[g, 2, high_rows], x_rec.at[g, 1], at_x(-1))
-        u_of(1)
-        xs[g, 1, 2] = message(u.at[g, 1, high_rows], x_rec.at[g, 2], at_x(1))
-        u_of(3)
-        xs[g, -1, 2] = message(u.at[g, 3, low_rows], x_rec.at[g, 3], at_x(-1))
-        u_of(0)
-
-    def x_second(g):
-        xs[g, 1, 1].wait_recv()
-        x_mer[g, 0] = u[g, 1, :HALF_ROWS] + x_rec[g, 0]
-        xs[g, 1, 3] = message(x_mer.at[g, 0], x_rec.at[g, 4], at_x(1))
-        xs[g, -1, 1].wait_recv()
-        x_mer[g, 1] = u[g, 3, HALF_ROWS:] + x_rec[g, 1]
-        xs[g, -1, 3] = message(x_mer.at[g, 1], x_rec.at[g, 5], at_x(-1))
-
-    zs = {}
-
-    def z_copy(g):
-        kk = group_of(g)
-        d = (kk - zh) % 4
-        slot = (d + 3) % 4
-        return d, pltpu.make_async_remote_copy(
-            src_ref=z_send.at[g], dst_ref=z_rec.at[slot],
-            send_sem=ssem.at[MESSAGES - 4 + g], recv_sem=rsem.at[MESSAGES - 4 + slot],
-            device_id={"dp": kk * 8 + x * 2 + c}, device_id_type=MESH,
+    waits = []
+
+    def has(i, d):
+        return (x + d) % 4 // 2 == order[i] % 2
+
+    def start_when(condition, *made):
+        waits.extend((condition, make) for make in made)
+        for make in made:
+            make().start()
+
+    X_SEM, Z_SEM = MESSAGES, MESSAGES + 48
+
+    def x_copy(i, kind, src, step):
+        sem = X_SEM + 6 * i + kind
+        return pltpu.make_async_remote_copy(
+            src_ref=src, dst_ref=x_rec.at[i, kind], send_sem=ssem.at[sem], recv_sem=rsem.at[sem],
+            device_id=at_x(step), device_id_type=MESH,
         )
 
-    def x_last(g):
-        for step in (1, -1):
-            xs[g, step, 2].wait_recv()
-            xs[g, step, 3].wait_recv()
-        upper = u[g, 0, :HALF_ROWS].astype(F32) + x_rec[g, 3].astype(F32) + x_rec[g, 4].astype(F32)
-        lower = u[g, 0, HALF_ROWS:].astype(F32) + x_rec[g, 2].astype(F32) + x_rec[g, 5].astype(F32)
-        z_send[g, :HALF_ROWS] = upper.astype(BF16)
-        z_send[g, HALF_ROWS:] = lower.astype(BF16)
-        d, copy = z_copy(g)
-
-        @pl.when(d != 0)
-        def _():
-            copy.start()
-
-        @pl.when(d == 0)
-        def _():
-            z_own[:HALF_ROWS] = upper
-            z_own[HALF_ROWS:] = lower
-
+    def x_far(i, src, step):
+        sem = X_SEM + 6 * i
+        return pltpu.make_async_remote_copy(
+            src_ref=src, dst_ref=x_rec.at[i, 0], send_sem=ssem.at[sem + (5 if step < 0 else 0)],
+            recv_sem=rsem.at[sem], device_id=at_x(step), device_id_type=MESH,
+        )
+
+    def z_copy(kind, src, step):
+        sem = Z_SEM + kind
+        return pltpu.make_async_remote_copy(
+            src_ref=src, dst_ref=z_rec.at[kind], send_sem=ssem.at[sem], recv_sem=rsem.at[sem],
+            device_id=at_zh(step), device_id_type=MESH,
+        )
+
+    def x_first(i):
+        cx[i].wait_recv()
+        u[i] = gwb[i, c] + cx_rec[i]
+        far, near, back_near = (x + 2) % 2, (x + 1) % 2, (x + 3) % 2
+        is_far, is_next, is_back = has(i, 2), has(i, 1), has(i, 3)
+
+        @pl.when(is_far)
+        def _():
+            start_when(
+                is_far,
+                lambda: x_far(i, u.at[i, far, low_rows], 1),
+                lambda: x_far(i, u.at[i, far, high_rows], -1),
+            )
+
+        @pl.when(is_next)
+        def _():
+            start_when(is_next, lambda: x_copy(i, 1, u.at[i, near, high_rows], 1))
+
+        @pl.when(is_back)
+        def _():
+            start_when(is_back, lambda: x_copy(i, 3, u.at[i, back_near, low_rows], -1))
+
+    def x_second(i):
+        near, back_near = (x + 1) % 2, (x + 3) % 2
+        is_next, is_back = has(i, 1), has(i, 3)
+
+        @pl.when(is_next)
+        def _():
+            x_far(i, x_mer.at[i], 1).wait_recv()
+            x_mer[i] = u[i, near, :HALF_ROWS] + x_rec[i, 0]
+            start_when(is_next, lambda: x_copy(i, 2, x_mer.at[i], 1))
+
+        @pl.when(is_back)
+        def _():
+            x_far(i, x_mer.at[i], -1).wait_recv()
+            x_mer[i] = u[i, back_near, HALF_ROWS:] + x_rec[i, 0]
+            start_when(is_back, lambda: x_copy(i, 4, x_mer.at[i], -1))
+
+    def x_last(i):
+        kk = order[i] // 2
+        e = (kk - zh) % 4
+        mine = has(i, 0)
+        is_far, is_next, is_back = mine & (e == 2), mine & (e == 1), mine & (e == 3)
+
+        @pl.when(mine)
+        def _():
+            for kind in (1, 2, 3, 4):
+                x_copy(i, kind, x_mer.at[i], 1).wait_recv()
+            upper = u[i, x % 2, :HALF_ROWS].astype(F32) + x_rec[i, 2].astype(F32) + x_rec[i, 3].astype(F32)
+            lower = u[i, x % 2, HALF_ROWS:].astype(F32) + x_rec[i, 1].astype(F32) + x_rec[i, 4].astype(F32)
+            z_send[i, :HALF_ROWS] = upper.astype(BF16)
+            z_send[i, HALF_ROWS:] = lower.astype(BF16)
+
+            @pl.when(e == 0)
+            def _():
+                z_own[:HALF_ROWS] = upper
+                z_own[HALF_ROWS:] = lower
+
+        @pl.when(is_far)
+        def _():
+            start_when(
+                is_far,
+                lambda: z_copy(0, z_send.at[i, low_rows], 1),
+                lambda: z_copy(1, z_send.at[i, high_rows], -1),
+            )
+
+        @pl.when(is_next)
+        def _():
+            start_when(is_next, lambda: z_copy(2, z_send.at[i, high_rows], 1))
+
+        @pl.when(is_back)
+        def _():
+            start_when(is_back, lambda: z_copy(4, z_send.at[i, low_rows], -1))
+
+    def z_second(i):
+        e = (order[i] // 2 - zh) % 4
+        is_next, is_back = has(i, 0) & (e == 1), has(i, 0) & (e == 3)
+
+        @pl.when(is_next)
+        def _():
+            z_copy(0, z_mer.at[0], 1).wait_recv()
+            z_mer[0] = z_send[i, :HALF_ROWS] + z_rec[0]
+            start_when(is_next, lambda: z_copy(3, z_mer.at[0], 1))
+
+        @pl.when(is_back)
+        def _():
+            z_copy(1, z_mer.at[1], -1).wait_recv()
+            z_mer[1] = z_send[i, HALF_ROWS:] + z_rec[1]
+            start_when(is_back, lambda: z_copy(5, z_mer.at[1], -1))
+
+    weight_grad(0)
     accumulate(lambda j: t, True)
     forward_on(all_a, z, y1, "a")
     forward_on(all_b, z, y1, "b")
@@ -384,52 +445,71 @@
     y2["b", -1, 1] = message(second_p, second_p, at_y(-1))
     y2["b", 1, 2] = message(second_p, second_p, at_y(1))
     y2["b", -1, 2] = message(first_p, first_p, at_y(-1))
+    x_first(0)
     y1["a", 1, 2].wait_recv()
     across(-1)
     y1["a", -1, 2].wait_recv()
     across(1)
+    zx_a[0].wait_recv()
+    weight_grad(1)
     gain_c.wait_recv()
     gain1[...] = gain0[...] + gain0_rec[...]
     gain_x = [message(gain1, gain1_rec.at[s - 1], at_x(s)) for s in (1, 2, 3)]
     y1["b", 1, 2].wait_recv()
     y1["b", -1, 2].wait_recv()
-    weight_grad(0)
-    x_first(0)
+    weight_grad(2)
+    weight_grad(3)
+    x_second(0)
+    x_first(1)
     y1["a", 1, 3].wait_recv()
     y1["a", -1, 3].wait_recv()
     across(2)
-    accumulate(lambda j: block_at(z, 1) * j + block_at(z, -1) * (1 - j), False)
-    x_second(0)
+    accumulate(lambda j: order[3] * j + order[2] * (1 - j), False)
+    x_second(1)
+    x_first(2)
+    x_first(3)
     y1["b", 1, 3].wait_recv()
     y1["b", -1, 3].wait_recv()
-    weight_grad(1)
-    x_first(1)
-    x_second(1)
+    weight_grad(4)
+    x_last(0)
+    accumulate(lambda j: order[4] * j + order[1] * (1 - j), False)
     forward_on(all_b, 1 - z, y2, "b")
-    zx_a[0].wait_recv()
-    accumulate(lambda j: block_at(z, 2) * j + block_at(1 - z, 0) * (1 - j), False)
+    x_second(2)
+    x_second(3)
+    x_first(4)
+    x_last(1)
+    z_second(0)
     for copy in gain_x:
         copy.wait_recv()
     gain2[...] = gain1[...] + gain1_rec[0] + gain1_rec[1] + gain1_rec[2]
     gain_z = [message(gain2, gain2_rec.at[s - 1], at_zh(s)) for s in (1, 2, 3)]
-    x_last(0)
     zx_a[-1].wait_recv()
     zx_a[1].wait_recv()
     y2["b", 1, 2].wait_recv()
     y2["b", -1, 2].wait_recv()
-    weight_grad(2)
-    x_first(2)
-    accumulate(lambda j: block_at(1 - z, 1) * j + block_at(1 - z, -1) * (1 - j), False)
+    weight_grad(5)
+    weight_grad(6)
+    x_second(4)
+    x_last(2)
+    z_second(1)
     zx_a[2].wait_recv()
     y2["b", 1, 3].wait_recv()
     y2["b", -1, 3].wait_recv()
-    weight_grad(3)
-    x_first(3)
-    x_second(2)
-    last = block_at(1 - z, 2)
+    weight_grad(7)
+    x_first(5)
+    x_first(6)
+    x_last(3)
+    accumulate(lambda j: order[6] * j + order[5] * (1 - j), False)
+    x_first(7)
+    x_second(5)
+    x_second(6)
+    x_last(4)
+    z_second(2)
+    z_second(3)
+    last = order[7]
     grad = jnp.concatenate([all_a[last], all_b[last]], axis=1)
     ga[...] = (gacc[...] + dot(grad, w[w_rows(last), :], 1, 0)).astype(BF16)
-    x_last(1)
+    x_second(7)
 
     def backward(h, carry):
         cols = head_cols(h)
@@ -444,45 +524,61 @@
         return carry
 
     lax.fori_loop(0, 2, backward, 0)
-    x_second(3)
+    x_last(5)
+    z_second(4)
     lax.fori_loop(2, 4, backward, 0)
-    x_last(2)
+    x_last(6)
+    z_second(5)
     lax.fori_loop(4, HEADS, backward, 0)
-    out_gq, out_gk, out_gv = fetch(gq, gq_hbm), fetch(gk, gk_hbm), fetch(gv, gv_hbm)
     for copy in gain_z:
         copy.wait_recv()
     gain = gain2[...] + gain2_rec[0] + gain2_rec[1] + gain2_rec[2]
-    gg_ref[...] = jnp.sum(gain, axis=0, keepdims=True)
-    x_last(3)
-
-    for slot in range(3):
-        pltpu.make_async_remote_copy(
-            src_ref=z_send.at[0], dst_ref=z_rec.at[slot],
-            send_sem=ssem.at[MESSAGES - 4], recv_sem=rsem.at[MESSAGES - 4 + slot],
-            device_id=c_peer, device_id_type=MESH,
-        ).wait_recv()
-    gw_out[...] = (
-        z_own[...] + z_rec[0].astype(F32) + z_rec[1].astype(F32) + z_rec[2].astype(F32)
-    )
-    out_gw = fetch(gw_out, gw_hbm)
+    gg_ref[...] = jnp.sum(gain, axis=0)
+    x_last(7)
+    z_second(6)
+    z_second(7)
+
+    for kind in (2, 3, 4, 5):
+        z_copy(kind, z_mer.at[0], 1).wait_recv()
+    gw_out[:HALF_ROWS] = z_own[:HALF_ROWS] + z_rec[3].astype(F32) + z_rec[4].astype(F32)
+    gw_out[HALF_ROWS:] = z_own[HALF_ROWS:] + z_rec[2].astype(F32) + z_rec[5].astype(F32)
 
     for copy in messages:
         copy.wait_send()
-    for g in range(4):
-        d, copy = z_copy(g)
-
-        @pl.when(d != 0)
-        def _():
-            copy.wait_send()
-
-    for copy in (out_lo, out_gr, out_gq, out_gk, out_gv, out_gw):
+    for condition, make in waits:
+
+        @pl.when(condition)
+        def _():
+            make().wait_send()
+
+    assert len(messages) <= MESSAGES
+
+
+def hand_over(*refs):
+    n = len(refs) // 2
+    sources, outs, sems = refs[:n], refs[n : 2 * n], refs[2 * n]
+    copies = [pltpu.make_async_copy(a, b, sems.at[i]) for i, (a, b) in enumerate(zip(sources, outs))]
+    for copy in copies:
+        copy.start()
+    for copy in copies:
         copy.wait()
-    assert len(messages) <= MESSAGES - 4
+
+
+def deliver(arrays):
+    vmem = pl.BlockSpec(memory_space=pltpu.VMEM)
+    return pl.pallas_call(
+        hand_over,
+        out_shape=[jax.ShapeDtypeStruct(a.shape, a.dtype) for a in arrays],
+        in_specs=[vmem] * len(arrays),
+        out_specs=[pl.BlockSpec(memory_space=pl.ANY)] * len(arrays),
+        scratch_shapes=[pltpu.SemaphoreType.DMA((len(arrays),))],
+        compiler_params=pltpu.CompilerParams(vmem_limit_bytes=8 << 20),
+    )(*arrays)
 
 
 def shards(q, k, v, mask, res, w, gain, ups, rg):
     rows = jax.ShapeDtypeStruct((LEN, WIDTH), BF16)
-    anywhere = pl.BlockSpec(memory_space=pl.ANY)
+    hbm = pl.BlockSpec(memory_space=pltpu.HBM)
     vmem = pl.BlockSpec(memory_space=pltpu.VMEM)
 
     def b(*shape):
@@ -495,17 +591,16 @@
     part = (OUT_ROWS, WIDTH)
     half = (HALF_ROWS, WIDTH)
     scratch = [
-        b(*slab), b(*slab), b(*slab), b(*slab), b(D, WIDTH), b(*slab), b(*slab),
-        f(LEN, LEN), f(HEADS, LEN, LEN), b(*slab), b(*slab), b(*slab), b(*slab), f(*slab),
-        b(*slab), b(*slab), b(*slab), f(*part),
+        b(*slab), b(*slab), b(*slab), pltpu.VMEM((1, LEN), jnp.int32), b(*slab), b(D, WIDTH), f(WIDTH), b(*slab), b(*slab),
+        f(LEN, LEN), f(HEADS, LEN, LEN), b(*slab), b(*slab), f(*slab),
         b(4, 2, LEN, CA), b(4, 2, LEN, CB), b(4, LEN, CA), b(6, HALF, CA), b(6, 2, HALF, CB),
         b(2, HALF, CA), b(2, 2, HALF, CB), b(LEN, CB), b(LEN, CB), f(*slab),
         f(8, LEN), f(8, 8, LEN), b(8, LEN, CA), b(8, LEN, CB),
-        b(4, 2, 4, *part), b(4, 4, *part), b(4, 4, *part), b(4, 6, *half), b(4, 2, *half),
-        b(4, *part), b(4, *part), f(*part),
+        b(8, 2, 2, *part), b(8, 2, *part), b(8, 2, *part), b(8, 5, *half), b(8, *half),
+        b(8, *part), b(6, *half), b(2, *half), f(*part),
         f(8, WIDTH), f(8, WIDTH), f(8, WIDTH), f(3, 8, WIDTH), f(8, WIDTH), f(3, 8, WIDTH),
-        pltpu.SemaphoreType.DMA((MESSAGES,)),
-        pltpu.SemaphoreType.DMA((MESSAGES,)),
+        pltpu.SemaphoreType.DMA((MESSAGES + 54,)),
+        pltpu.SemaphoreType.DMA((MESSAGES + 54,)),
         pltpu.SemaphoreType.DMA((16,)),
     ]
     outs = pl.pallas_call(
@@ -513,16 +608,16 @@
         out_shape=(
             rows, rows, rows, rows, rows,
             jax.ShapeDtypeStruct(part, F32),
-            jax.ShapeDtypeStruct((1, WIDTH), F32),
+            jax.ShapeDtypeStruct((WIDTH,), F32),
         ),
-        in_specs=[anywhere, anywhere, anywhere, vmem, anywhere, anywhere, vmem, anywhere, anywhere],
-        out_specs=(anywhere,) * 6 + (vmem,),
+        in_specs=[hbm] * 9,
+        out_specs=(vmem,) * 7,
         scratch_shapes=scratch,
         compiler_params=pltpu.CompilerParams(
-            collective_id=0, has_side_effects=True, vmem_limit_bytes=64000000
+            collective_id=0, has_side_effects=True, vmem_limit_bytes=VMEM_LIMIT
         ),
-    )(q, k, v, mask, res, w, gain.reshape(1, WIDTH), ups, rg)
-    return (*outs[:6], outs[6].reshape(WIDTH))
+    )(q, k, v, mask, res, w, gain, ups, rg)
+    return deliver(outs)
 
 
 def solution(mesh):

time: 130 us -> 116 us (0.89)
  local copies, waits for them, and re-layouts: 12.3 us -> 1.36 us
  Pallas kernels: 116 us -> 113 us
    unnamed x6 -> x4, local copies, waits for them, and re-layouts: 11 us -> 1.36 us
    pallas_call x1, Pallas kernels: 116 us -> 112 us  [shards(): pl.pallas_call(kernel, out_shape=(rows, rows, rows, rows, rows, jax.Shape...]
    pallas_call x0 -> x1, Pallas kernels: none -> 1.63 us  [deliver(): pl.pallas_call(hand_over, out_shape=[jax.ShapeDtypeStruct(a.shape, a.dtyp...]
where the time goes in v2:
time: 116 us
  Pallas kernels  113 us (97%)
  local copies, waits for them, and re-layouts  1.36 us (1%)
    pallas_call x1, Pallas kernels, shards(): pl.pallas_call(kernel, out_shape=(rows, rows, rows, rows, rows, jax.Shape...  112 us

profile of v2, /device:TPU:56, one launch (start us, length us, event | category | flops | bytes accessed | tf_op | source)
XLA Modules:
  0.0 115.6 jit_solution(15569968538269275369)
XLA Ops:
  0.6 0.0 copy-start
  0.6 0.7 copy-done
  1.3 0.0 copy-start.1
  1.3 0.7 copy-done.1
  2.0 111.8 %shard_map.144 = (bf16[384,640]{1,0:T(8,128)(2,1)S(1)}, bf16[384,640]{1,0:T(8,128)(2,1)S(1)}, bf16[384,640]{1,0:T(8,128)(2,1)S(1)}, bf16[384,640]{1,0:T(8,128)(2...) custom-call(bf16[384,640]{1,0:T(8,128)(2,1)} %q_hbm.1, bf16[384,640]{1,0:T(8,128)(2,1)} %k_hbm.1, ...), custom_call_target="tpu_custom_call" | custom-call | tf_op jit(solution)/shard_map/pallas_call | solution.py:606
  113.8 1.6 %shard_map.145 = (bf16[384,640]{1,0:T(8,128)(2,1)}, bf16[384,640]{1,0:T(8,128)(2,1)}, bf16[384,640]{1,0:T(8,128)(2,1)}, bf16[384,640]{1,0:T(8,128)(2,1)}, bf16[3...) custom-call(bf16[384,640]{1,0:T(8,128)(2,1)S(1)} %get-tuple-element.14.refs_0_, ...), custom_call_target="tpu_custom_call" | custom-call | tf_op jit(solution)/shard_map/pallas_call | solution.py:569
Async XLA Ops:
  0.6 0.7 copy-start
  1.3 0.7 copy-start.1

commit v3 on v2

--- a/solution.py
+++ b/solution.py
@@ -19,6 +19,7 @@
 CA = 256
 CB = WIDTH - CA
 HALF = LEN // 2
+QUARTER = HALF // 2
 OUT_ROWS = 160
 HALF_ROWS = OUT_ROWS // 2
 SCALE = HEAD_DIM ** (-0.5)
@@ -107,182 +108,199 @@
     def head_cols(h):
         return pl.ds(pl.multiple_of(h * HEAD_DIM, HEAD_DIM), HEAD_DIM)
 
-    def forward(h, carry):
-        cols = head_cols(h)
-        s = dot(q[:, cols], k[:, cols], 1, 1) * SCALE + bias[...]
-        e = jnp.exp(s - jnp.max(s, axis=1, keepdims=True))
-        p = e * (1.0 / jnp.sum(e, axis=1, keepdims=True))
-        probs[h] = p
-        att[:, cols] = dot(p.astype(BF16), v[:, cols], 1, 0).astype(BF16)
-        return carry
-
-    lax.fori_loop(0, HEADS, forward, 0)
-    in_w.wait()
+    units = (pl.ds(0, HALF), pl.ds(HALF, HALF))
+    firsts = (pl.ds(0, QUARTER), pl.ds(HALF, QUARTER))
+    seconds = (pl.ds(QUARTER, QUARTER), pl.ds(HALF + QUARTER, QUARTER))
+
+    def attend(n):
+        rows = units[n]
+
+        def forward(h, carry):
+            cols = head_cols(h)
+            s = dot(q[rows, cols], k[:, cols], 1, 1) * SCALE + bias[rows]
+            e = jnp.exp(s - jnp.max(s, axis=1, keepdims=True))
+            p = e * (1.0 / jnp.sum(e, axis=1, keepdims=True))
+            probs[h, rows] = p
+            att[rows, cols] = dot(p.astype(BF16), v[:, cols], 1, 0).astype(BF16)
+            return carry
+
+        lax.fori_loop(0, HEADS, forward, 0, unroll=True)
 
     def w_rows(block):
         return pl.ds(pl.multiple_of(block * WIDTH, WIDTH), WIDTH)
 
-    def project(d):
+    def project(n, d):
+        rows = units[n]
+
         def one(j, carry):
             zz = j * z + (1 - j) * (1 - z)
             block = zz * 4 + (y + d) % 4
-            r = dot(att[...], w[w_rows(block), :], 1, 1)
-            pa[d, j] = r[:, :CA].astype(BF16)
-            pb[d, zz] = r[:, CA:].astype(BF16)
+            r = dot(att[rows], w[w_rows(block), :], 1, 1)
+            pa[d, j, rows] = r[:, :CA].astype(BF16)
+            pb[d, zz, rows] = r[:, CA:].astype(BF16)
             return carry
 
         lax.fori_loop(0, 2, one, 0)
 
-    first, second = pl.ds(0, HALF), pl.ds(HALF, HALF)
-    az, b1, b2, a1, a2 = {}, {}, {}, {}, {}
-    project(2)
-    pl.semaphore_wait(barrier, len(peers))
-    b1[1] = message(pb.at[2, :, first], rec_b.at[0], at_y(1))
-    b1[-1] = message(pb.at[2, :, second], rec_b.at[1], at_y(-1))
-    az[2] = message(pa.at[2, 0], rec_az.at[2], z_peer)
-    project(1)
-    b2[1] = message(pb.at[1, :, second], rec_b.at[2], at_y(1))
-    az[1] = message(pa.at[1, 0], rec_az.at[1], z_peer)
-    project(3)
-    b2[-1] = message(pb.at[3, :, first], rec_b.at[3], at_y(-1))
-    az[3] = message(pa.at[3, 0], rec_az.at[3], z_peer)
-    project(0)
-    az[0] = message(pa.at[0, 0], rec_az.at[0], z_peer)
-
-    b1[1].wait_recv()
-    mer_b[0] = pb[1, :, :HALF] + rec_b[0]
-    b3 = {1: message(mer_b.at[0], rec_b.at[4], at_y(1))}
-    b1[-1].wait_recv()
-    mer_b[1] = pb[3, :, HALF:] + rec_b[1]
-    b3[-1] = message(mer_b.at[1], rec_b.at[5], at_y(-1))
-
-    def join(d):
-        az[d].wait_recv()
-        pa[d, 1] = pa[d, 1] + rec_az[d]
-
-    join(2)
-    a1[1] = message(pa.at[2, 1, first], rec_a.at[0], at_y(1))
-    a1[-1] = message(pa.at[2, 1, second], rec_a.at[1], at_y(-1))
-    join(1)
-    a2[1] = message(pa.at[1, 1, second], rec_a.at[2], at_y(1))
-    join(3)
-    a2[-1] = message(pa.at[3, 1, first], rec_a.at[3], at_y(-1))
-    az[0].wait_recv()
-
-    b2[1].wait_recv()
-    b2[-1].wait_recv()
-    b3[1].wait_recv()
-    b3[-1].wait_recv()
-
-    def b_sum(zz):
-        top = pb[0, zz, :HALF].astype(F32) + rec_b[3, zz].astype(F32) + rec_b[4, zz].astype(F32)
-        low = pb[0, zz, HALF:].astype(F32) + rec_b[2, zz].astype(F32) + rec_b[5, zz].astype(F32)
+    rs = {}
+
+    def send_far(n):
+        rs["b", n, 0] = message(pb.at[2, :, firsts[n]], rec_b.at[n, 0], at_y(1))
+        rs["b", n, 1] = message(pb.at[2, :, seconds[n]], rec_b.at[n, 1], at_y(-1))
+
+    def send_up(n):
+        rs["b", n, 2] = message(pb.at[1, :, seconds[n]], rec_b.at[n, 2], at_y(1))
+
+    def send_down(n):
+        rs["b", n, 3] = message(pb.at[3, :, firsts[n]], rec_b.at[n, 3], at_y(-1))
+
+    def send_z(n, d):
+        rs["z", n, d] = message(pa.at[d, 0, units[n]], rec_az.at[d, units[n]], z_peer)
+
+    def merge_b(n):
+        rs["b", n, 0].wait_recv()
+        mer_b[n, 0] = pb[1, :, firsts[n]] + rec_b[n, 0]
+        rs["b", n, 4] = message(mer_b.at[n, 0], rec_b.at[n, 4], at_y(1))
+        rs["b", n, 1].wait_recv()
+        mer_b[n, 1] = pb[3, :, seconds[n]] + rec_b[n, 1]
+        rs["b", n, 5] = message(mer_b.at[n, 1], rec_b.at[n, 5], at_y(-1))
+
+    def join(n, d):
+        rs["z", n, d].wait_recv()
+        pa[d, 1, units[n]] = pa[d, 1, units[n]] + rec_az[d, units[n]]
+
+    def join_far(n):
+        join(n, 2)
+        rs["a", n, 0] = message(pa.at[2, 1, firsts[n]], rec_a.at[n, 0], at_y(1))
+        rs["a", n, 1] = message(pa.at[2, 1, seconds[n]], rec_a.at[n, 1], at_y(-1))
+
+    def join_up(n):
+        join(n, 1)
+        rs["a", n, 2] = message(pa.at[1, 1, seconds[n]], rec_a.at[n, 2], at_y(1))
+
+    def join_down(n):
+        join(n, 3)
+        rs["a", n, 3] = message(pa.at[3, 1, firsts[n]], rec_a.at[n, 3], at_y(-1))
+
+    def merge_a(n):
+        rs["a", n, 0].wait_recv()
+        mer_a[n, 0] = pa[1, 1, firsts[n]] + rec_a[n, 0]
+        rs["a", n, 4] = message(mer_a.at[n, 0], rec_a.at[n, 4], at_y(1))
+        rs["a", n, 1].wait_recv()
+        mer_a[n, 1] = pa[3, 1, seconds[n]] + rec_a[n, 1]
+        rs["a", n, 5] = message(mer_a.at[n, 1], rec_a.at[n, 5], at_y(-1))
+
+    def b_sum(n, zz):
+        top = pb[0, zz, firsts[n]].astype(F32) + rec_b[n, 3, zz].astype(F32) + rec_b[n, 4, zz].astype(F32)
+        low = pb[0, zz, seconds[n]].astype(F32) + rec_b[n, 2, zz].astype(F32) + rec_b[n, 5, zz].astype(F32)
         return top, low
 
-    top, low = b_sum(1 - z)
-    zb_send[:HALF] = top.astype(BF16)
-    zb_send[HALF:] = low.astype(BF16)
-    zb = message(zb_send, zb_rec, z_peer)
-
-    a1[1].wait_recv()
-    mer_a[0] = pa[1, 1, :HALF] + rec_a[0]
-    a3 = {1: message(mer_a.at[0], rec_a.at[4], at_y(1))}
-    a1[-1].wait_recv()
-    mer_a[1] = pa[3, 1, HALF:] + rec_a[1]
-    a3[-1] = message(mer_a.at[1], rec_a.at[5], at_y(-1))
-
-    in_res.wait()
-    in_ups.wait()
-    in_gain.wait()
-    gain_row = gain_ref[...].reshape(1, WIDTH)
-    in_rg.wait()
-    top, low = b_sum(z)
-    own[:HALF, CA:] = top
-    own[HALF:, CA:] = low
-    own[:, :CA] = pa[0, 1].astype(F32) + rec_az[0].astype(F32)
-
-    zb.wait_recv()
-    own_b = own[:, CA:] + zb_rec[...].astype(F32) + res[:, CA:].astype(F32)
-    low_b = own_b.astype(BF16)
-    lo[:, CA:] = low_b
-    f_b = low_b.astype(F32)
-    scaled_b = ups[:, CA:].astype(F32) * gain_row[:, CA:]
-    square = jnp.sum(f_b * f_b, axis=1, keepdims=True)
-    inner = jnp.sum(f_b * scaled_b, axis=1, keepdims=True)
-
-    a2[1].wait_recv()
-    a2[-1].wait_recv()
-    a3[1].wait_recv()
-    a3[-1].wait_recv()
-    top = own[:HALF, :CA] + rec_a[3].astype(F32) + rec_a[4].astype(F32) + res[:HALF, :CA].astype(F32)
-    low = own[HALF:, :CA] + rec_a[2].astype(F32) + rec_a[5].astype(F32) + res[HALF:, :CA].astype(F32)
-    lo[:HALF, :CA] = top.astype(BF16)
-    lo[HALF:, :CA] = low.astype(BF16)
-    f_a = lo[:, :CA].astype(F32)
-    scaled_a = ups[:, :CA].astype(F32) * gain_row[:, :CA]
-    square = square + jnp.sum(f_a * f_a, axis=1, keepdims=True)
-    inner = inner + jnp.sum(f_a * scaled_a, axis=1, keepdims=True)
-
-    lane = lax.broadcasted_iota(jnp.int32, (LEN, 128), 1)
-    packed = jnp.where(lane == 0, square, jnp.where(lane == 1, inner, 0.0))
-    stat[...] = packed.T[:8]
-    stats = [message(stat, stat_rec.at[j], peers[j - 1]) for j in range(1, 8)]
-    total = stat[...]
-    for j in range(1, 8):
-        stats[j - 1].wait_recv()
-        total = total + stat_rec[j]
-    wide = jnp.concatenate([total, jnp.zeros((120, LEN), F32)], axis=0).T
-    square, inner = wide[:, 0:1], wide[:, 1:2]
-    rms = jnp.sqrt(square / D + EPSILON)
-    back = 1.0 / rms
-    row_inner = inner / (rms * D)
-
-    def grad_rows(lo_part, ups_part, gain_part, rg_part):
-        up = ups_part.astype(F32)
-        normed = lo_part.astype(F32) * back
-        g = rg_part.astype(F32) + (up * gain_part - normed * row_inner) * back
-        return g.astype(BF16), (up * normed).reshape(LEN // 8, 8, -1).sum(axis=0)
-
-    g, gain_a = grad_rows(lo[:, :CA], ups[:, :CA], gain_row[:, :CA], rg[:, :CA])
-    all_a[t] = g
-    gr[:, :CA] = g
-    mine_a = all_a.at[t]
-    first_a = all_a.at[t, first]
-    second_a = all_a.at[t, second]
-    y1 = {}
-    y1["a", 1, 1] = message(first_a, first_a, at_y(1))
-    y1["a", -1, 1] = message(second_a, second_a, at_y(-1))
-    g, gain_b = grad_rows(lo[:, CA:], ups[:, CA:], gain_row[:, CA:], rg[:, CA:])
-    all_b[t] = g
-    gr[:, CA:] = g
-    zx_b = message(all_b.at[t], all_b.at[t], z_peer)
-    zx_a = {0: message(mine_a, mine_a, z_peer)}
-    first_b = all_b.at[t, first]
-    second_b = all_b.at[t, second]
-    y1["b", 1, 1] = message(first_b, first_b, at_y(1))
-    y1["b", -1, 1] = message(second_b, second_b, at_y(-1))
-    y1["a", 1, 2] = message(second_a, second_a, at_y(1))
-    y1["a", -1, 2] = message(first_a, first_a, at_y(-1))
-    y1["b", 1, 2] = message(second_b, second_b, at_y(1))
-    y1["b", -1, 2] = message(first_b, first_b, at_y(-1))
-    gain0[:, :CA] = gain_a
-    gain0[:, CA:] = gain_b
-    gain_c = message(gain0, gain0_rec, c_peer)
+    def cross_b(n):
+        for i in (2, 3, 4, 5):
+            rs["b", n, i].wait_recv()
+        top, low = b_sum(n, 1 - z)
+        zb_send[firsts[n]] = top.astype(BF16)
+        zb_send[seconds[n]] = low.astype(BF16)
+        rs["zb", n] = message(zb_send.at[units[n]], zb_rec.at[units[n]], z_peer)
+        top, low = b_sum(n, z)
+        own[firsts[n], CA:] = top
+        own[seconds[n], CA:] = low
+
+    def finish(n):
+        rows = units[n]
+        rs["z", n, 0].wait_recv()
+        for i in (2, 3, 4, 5):
+            rs["a", n, i].wait_recv()
+        add_top = rec_a[n, 3].astype(F32) + rec_a[n, 4].astype(F32)
+        add_low = rec_a[n, 2].astype(F32) + rec_a[n, 5].astype(F32)
+        for part, add in ((firsts[n], add_top), (seconds[n], add_low)):
+            total = pa[0, 1, part].astype(F32) + rec_az[0, part].astype(F32) + add
+            lo[part, :CA] = (total + res[part, :CA].astype(F32)).astype(BF16)
+        f_a = lo[rows, :CA].astype(F32)
+        scaled_a = ups[rows, :CA].astype(F32) * gain_row[:, :CA]
+        square = jnp.sum(f_a * f_a, axis=1, keepdims=True)
+        inner = jnp.sum(f_a * scaled_a, axis=1, keepdims=True)
+        rs["zb", n].wait_recv()
+        own_b = own[rows, CA:] + zb_rec[rows].astype(F32) + res[rows, CA:].astype(F32)
+        low_b = own_b.astype(BF16)
+        lo[rows, CA:] = low_b
+        f_b = low_b.astype(F32)
+        scaled_b = ups[rows, CA:].astype(F32) * gain_row[:, CA:]
+        square = square + jnp.sum(f_b * f_b, axis=1, keepdims=True)
+        inner = inner + jnp.sum(f_b * scaled_b, axis=1, keepdims=True)
+        lane = lax.broadcasted_iota(jnp.int32, (HALF, 128), 1)
+        packed = jnp.where(lane == 0, square, jnp.where(lane == 1, inner, 0.0))
+        packed = jnp.concatenate([packed, jnp.zeros((64, 128), F32)], axis=0)
+        stat[n] = packed.T[:8]
+        for j in range(1, 8):
+            rs["s", n, j] = message(stat.at[n], stat_rec.at[n, j], peers[j - 1])
+
+    ag = {}
+
+    def gradient(n):
+        rows = units[n]
+        total = stat[n]
+        for j in range(1, 8):
+            rs["s", n, j].wait_recv()
+            total = total + stat_rec[n, j]
+        wide = jnp.concatenate([total, jnp.zeros((120, 256), F32)], axis=0).T[:HALF]
+        square, inner = wide[:, 0:1], wide[:, 1:2]
+        rms = jnp.sqrt(square / D + EPSILON)
+        back = 1.0 / rms
+        row_inner = inner / (rms * D)
+        cut = (slice(0, CA), slice(CA, WIDTH))
+        for buf, cols in zip((all_a, all_b), cut):
+            up = ups[rows, cols].astype(F32)
+            normed = lo[rows, cols].astype(F32) * back
+            g = rg[rows, cols].astype(F32) + (up * gain_row[:, cols] - normed * row_inner) * back
+            g = g.astype(BF16)
+            buf[t, rows] = g
+            gr[rows, cols] = g
+            share = (up * normed).reshape(HALF // 8, 8, -1).sum(axis=0)
+            if n == 0:
+                gain0[:, cols] = share
+            else:
+                gain0[:, cols] += share
+        ag["zb", n] = message(all_b.at[t, rows], all_b.at[t, rows], z_peer)
+        for key, buf in (("a", all_a), ("b", all_b)):
+            send_half(key, buf, t, n, 1, firsts[n], 1)
+            send_half(key, buf, t, n, -1, seconds[n], 1)
+
+    def send_rest(n):
+        rows = units[n]
+        ag["za", n, 0] = message(all_a.at[t, rows], all_a.at[t, rows], z_peer)
+        for key, buf in (("a", all_a), ("b", all_b)):
+            send_half(key, buf, t, n, 1, seconds[n], 2)
+            send_half(key, buf, t, n, -1, firsts[n], 2)
+
+    def send_half(key, buf, block, n, step, rows, turn):
+        part = buf.at[block, rows]
+        ag[key, n, step, turn] = message(part, part, at_y(step))
 
     def block_at(zz, step):
         return zz * 4 + (y + step) % 4
 
-    def forward_on(buf, zz, sent, key):
-        sent[key, 1, 1].wait_recv()
-        part = buf.at[block_at(zz, -1), first]
-        sent[key, 1, 3] = message(part, part, at_y(1))
-        sent[key, -1, 1].wait_recv()
-        part = buf.at[block_at(zz, 1), second]
-        sent[key, -1, 3] = message(part, part, at_y(-1))
-
-    def across(step):
-        part = all_a.at[block_at(z, step)]
-        zx_a[step] = message(part, part, z_peer)
+    def forward_on(key, buf, zz, n):
+        ag[key, n, 1, 1].wait_recv()
+        send_half(key, buf, block_at(zz, -1), n, 1, firsts[n], 3)
+        ag[key, n, -1, 1].wait_recv()
+        send_half(key, buf, block_at(zz, 1), n, -1, seconds[n], 3)
+
+    def arrived(key, n, turn):
+        ag[key, n, 1, turn].wait_recv()
+        ag[key, n, -1, turn].wait_recv()
+
+    def partner(n):
+        ag["zb", n].wait_recv()
+        block = block_at(1 - z, 0)
+        send_half("p", all_b, block, n, 1, firsts[n], 1)
+        send_half("p", all_b, block, n, -1, seconds[n], 1)
+        send_half("p", all_b, block, n, 1, seconds[n], 2)
+        send_half("p", all_b, block, n, -1, firsts[n], 2)
+
+    def across(step, n):
+        part = all_a.at[block_at(z, step), units[n]]
+        ag["za", n, step] = message(part, part, z_peer)
 
     def accumulate(blocks, start):
         def one(j, carry):
@@ -297,6 +315,59 @@
 
         lax.fori_loop(0, 1 if start else 2, one, 0)
 
+    attend(0)
+    in_w.wait()
+    project(0, 2)
+    pl.semaphore_wait(barrier, len(peers))
+    send_far(0)
+    send_z(0, 2)
+    project(0, 1)
+    send_up(0)
+    send_z(0, 1)
+    project(0, 3)
+    send_down(0)
+    send_z(0, 3)
+    project(0, 0)
+    send_z(0, 0)
+    attend(1)
+    project(1, 2)
+    merge_b(0)
+    send_far(1)
+    send_z(1, 2)
+    join_far(0)
+    project(1, 1)
+    send_up(1)
+    send_z(1, 1)
+    project(1, 3)
+    send_down(1)
+    join_up(0)
+    join_down(0)
+    project(1, 0)
+    in_res.wait()
+    in_ups.wait()
+    in_gain.wait()
+    in_rg.wait()
+    gain_row = gain_ref[...].reshape(1, WIDTH)
+    cross_b(0)
+    send_z(1, 3)
+    send_z(1, 0)
+    merge_a(0)
+    merge_b(1)
+    join_far(1)
+    join_up(1)
+    finish(0)
+    join_down(1)
+    cross_b(1)
+    merge_a(1)
+    gradient(0)
+    finish(1)
+    send_rest(0)
+    forward_on("a", all_a, z, 0)
+    forward_on("b", all_b, z, 0)
+    gradient(1)
+    send_rest(1)
+    gain_c = message(gain0, gain0_rec, c_peer)
+
     order = [t, block_at(1 - z, 0), block_at(z, -1), block_at(z, 1), block_at(z, 2)]
     order += [block_at(1 - z, -1), block_at(1 - z, 1), block_at(1 - z, 2)]
     cx = {}
@@ -433,82 +504,77 @@
             start_when(is_back, lambda: z_copy(5, z_mer.at[1], -1))
 
     weight_grad(0)
-    accumulate(lambda j: t, True)
-    forward_on(all_a, z, y1, "a")
-    forward_on(all_b, z, y1, "b")
-    zx_b.wait_recv()
-    y2 = {}
-    other = block_at(1 - z, 0)
-    first_p = all_b.at[other, first]
-    second_p = all_b.at[other, second]
-    y2["b", 1, 1] = message(first_p, first_p, at_y(1))
-    y2["b", -1, 1] = message(second_p, second_p, at_y(-1))
-    y2["b", 1, 2] = message(second_p, second_p, at_y(1))
-    y2["b", -1, 2] = message(first_p, first_p, at_y(-1))
+    arrived("a", 0, 2)
+    across(-1, 0)
+    across(1, 0)
+    partner(0)
+    forward_on("a", all_a, z, 1)
+    arrived("a", 0, 3)
+    across(2, 0)
+    forward_on("b", all_b, z, 1)
+    partner(1)
     x_first(0)
-    y1["a", 1, 2].wait_recv()
-    across(-1)
-    y1["a", -1, 2].wait_recv()
-    across(1)
-    zx_a[0].wait_recv()
+    arrived("a", 1, 2)
+    across(-1, 1)
+    across(1, 1)
+    arrived("b", 0, 2)
+    arrived("b", 1, 2)
+    weight_grad(2)
+    weight_grad(3)
+    forward_on("p", all_b, 1 - z, 0)
+    x_first(2)
+    x_first(3)
+    ag["za", 0, 0].wait_recv()
+    ag["za", 1, 0].wait_recv()
     weight_grad(1)
     gain_c.wait_recv()
     gain1[...] = gain0[...] + gain0_rec[...]
     gain_x = [message(gain1, gain1_rec.at[s - 1], at_x(s)) for s in (1, 2, 3)]
-    y1["b", 1, 2].wait_recv()
-    y1["b", -1, 2].wait_recv()
-    weight_grad(2)
-    weight_grad(3)
     x_second(0)
+    accumulate(lambda j: t, True)
     x_first(1)
-    y1["a", 1, 3].wait_recv()
-    y1["a", -1, 3].wait_recv()
-    across(2)
+    arrived("a", 1, 3)
+    across(2, 1)
+    arrived("b", 0, 3)
+    arrived("b", 1, 3)
+    weight_grad(4)
+    forward_on("p", all_b, 1 - z, 1)
     accumulate(lambda j: order[3] * j + order[2] * (1 - j), False)
+    x_second(2)
+    x_first(4)
+    x_second(3)
+    for n in (0, 1):
+        ag["za", n, -1].wait_recv()
+        ag["za", n, 1].wait_recv()
+        arrived("p", n, 2)
+    weight_grad(5)
+    weight_grad(6)
     x_second(1)
-    x_first(2)
-    x_first(3)
-    y1["b", 1, 3].wait_recv()
-    y1["b", -1, 3].wait_recv()
-    weight_grad(4)
     x_last(0)
+    x_first(5)
+    x_first(6)
     accumulate(lambda j: order[4] * j + order[1] * (1 - j), False)
-    forward_on(all_b, 1 - z, y2, "b")
-    x_second(2)
-    x_second(3)
-    x_first(4)
-    x_last(1)
-    z_second(0)
+    for n in (0, 1):
+        ag["za", n, 2].wait_recv()
+        arrived("p", n, 3)
+    weight_grad(7)
+    x_second(4)
+    x_last(2)
+    x_first(7)
     for copy in gain_x:
         copy.wait_recv()
     gain2[...] = gain1[...] + gain1_rec[0] + gain1_rec[1] + gain1_rec[2]
     gain_z = [message(gain2, gain2_rec.at[s - 1], at_zh(s)) for s in (1, 2, 3)]
-    zx_a[-1].wait_recv()
-    zx_a[1].wait_recv()
-    y2["b", 1, 2].wait_recv()
-    y2["b", -1, 2].wait_recv()
-    weight_grad(5)
-    weight_grad(6)
-    x_second(4)
-    x_last(2)
-    z_second(1)
-    zx_a[2].wait_recv()
-    y2["b", 1, 3].wait_recv()
-    y2["b", -1, 3].wait_recv()
-    weight_grad(7)
-    x_first(5)
-    x_first(6)
+    x_last(1)
+    accumulate(lambda j: order[6] * j + order[5] * (1 - j), False)
     x_last(3)
-    accumulate(lambda j: order[6] * j + order[5] * (1 - j), False)
-    x_first(7)
     x_second(5)
-    x_second(6)
-    x_last(4)
-    z_second(2)
-    z_second(3)
     last = order[7]
     grad = jnp.concatenate([all_a[last], all_b[last]], axis=1)
     ga[...] = (gacc[...] + dot(grad, w[w_rows(last), :], 1, 0)).astype(BF16)
+    x_last(4)
+    x_second(6)
+    z_second(0)
     x_second(7)
 
     def backward(h, carry):
@@ -524,17 +590,20 @@
         return carry
 
     lax.fori_loop(0, 2, backward, 0)
+    z_second(2)
+    z_second(1)
     x_last(5)
-    z_second(4)
-    lax.fori_loop(2, 4, backward, 0)
+    lax.fori_loop(2, 3, backward, 0)
     x_last(6)
-    z_second(5)
-    lax.fori_loop(4, HEADS, backward, 0)
+    x_last(7)
+    lax.fori_loop(3, HEADS, backward, 0)
     for copy in gain_z:
         copy.wait_recv()
     gain = gain2[...] + gain2_rec[0] + gain2_rec[1] + gain2_rec[2]
     gg_ref[...] = jnp.sum(gain, axis=0)
-    x_last(7)
+    z_second(3)
+    z_second(4)
+    z_second(5)
     z_second(6)
     z_second(7)
 
@@ -593,9 +662,9 @@
     scratch = [
         b(*slab), b(*slab), b(*slab), pltpu.VMEM((1, LEN), jnp.int32), b(*slab), b(D, WIDTH), f(WIDTH), b(*slab), b(*slab),
         f(LEN, LEN), f(HEADS, LEN, LEN), b(*slab), b(*slab), f(*slab),
-        b(4, 2, LEN, CA), b(4, 2, LEN, CB), b(4, LEN, CA), b(6, HALF, CA), b(6, 2, HALF, CB),
-        b(2, HALF, CA), b(2, 2, HALF, CB), b(LEN, CB), b(LEN, CB), f(*slab),
-        f(8, LEN), f(8, 8, LEN), b(8, LEN, CA), b(8, LEN, CB),
+        b(4, 2, LEN, CA), b(4, 2, LEN, CB), b(4, LEN, CA), b(2, 6, QUARTER, CA), b(2, 6, 2, QUARTER, CB),
+        b(2, 2, QUARTER, CA), b(2, 2, 2, QUARTER, CB), b(LEN, CB), b(LEN, CB), f(*slab),
+        f(2, 8, 256), f(2, 8, 8, 256), b(8, LEN, CA), b(8, LEN, CB),
         b(8, 2, 2, *part), b(8, 2, *part), b(8, 2, *part), b(8, 5, *half), b(8, *half),
         b(8, *part), b(6, *half), b(2, *half), f(*part),
         f(8, WIDTH), f(8, WIDTH), f(8, WIDTH), f(3, 8, WIDTH), f(8, WIDTH), f(3, 8, WIDTH),

time: 116 us -> 107 us (0.922)
  Pallas kernels: 113 us -> 104 us
    pallas_call x1, Pallas kernels: 112 us -> 103 us  [shards(): pl.pallas_call(kernel, out_shape=(rows, rows, rows, rows, rows, jax.Shape...]
where the time goes in v3:
time: 107 us; the launch traced here: 106 us
  Pallas kernels  104 us (97%)
  local copies, waits for them, and re-layouts  1.36 us (1%)
    pallas_call x1, Pallas kernels, shards(): pl.pallas_call(kernel, out_shape=(rows, rows, rows, rows, rows, jax.Shape...  103 us

profile of v3, /device:TPU:56, one launch (start us, length us, event | category | flops | bytes accessed | tf_op | source)
XLA Modules:
  0.0 106.4 jit_solution(2750185147800830230)
XLA Ops:
  0.6 0.0 copy-start
  0.6 0.7 copy-done
  1.3 0.0 copy-start.1
  1.3 0.7 copy-done.1
  2.0 102.6 %shard_map.144 = (bf16[384,640]{1,0:T(8,128)(2,1)S(1)}, bf16[384,640]{1,0:T(8,128)(2,1)S(1)}, bf16[384,640]{1,0:T(8,128)(2,1)S(1)}, bf16[384,640]{1,0:T(8,128)(2...) custom-call(bf16[384,640]{1,0:T(8,128)(2,1)} %q_hbm.1, bf16[384,640]{1,0:T(8,128)(2,1)} %k_hbm.1, ...), custom_call_target="tpu_custom_call" | custom-call | tf_op jit(solution)/shard_map/pallas_call | solution.py:675
  104.7 1.6 %shard_map.145 = (bf16[384,640]{1,0:T(8,128)(2,1)}, bf16[384,640]{1,0:T(8,128)(2,1)}, bf16[384,640]{1,0:T(8,128)(2,1)}, bf16[384,640]{1,0:T(8,128)(2,1)}, bf16[3...) custom-call(bf16[384,640]{1,0:T(8,128)(2,1)S(1)} %get-tuple-element.14.refs_0_, ...), custom_call_target="tpu_custom_call" | custom-call | tf_op jit(solution)/shard_map/pallas_call | solution.py:638
Async XLA Ops:
  0.6 0.7 copy-start
  1.3 0.7 copy-start.1

commit v4 on v3

--- a/solution.py
+++ b/solution.py
@@ -385,10 +385,17 @@
     def has(i, d):
         return (x + d) % 4 // 2 == order[i] % 2
 
-    def start_when(condition, *made):
-        waits.extend((condition, make) for make in made)
+    z_waits = []
+
+    def start_when(condition, *made, held=waits):
+        held.extend((condition, make) for make in made)
         for make in made:
             make().start()
+
+    def wait_when(condition, make):
+        @pl.when(condition)
+        def _():
+            make().wait_send()
 
     X_SEM, Z_SEM = MESSAGES, MESSAGES + 48
 
@@ -477,15 +484,16 @@
                 is_far,
                 lambda: z_copy(0, z_send.at[i, low_rows], 1),
                 lambda: z_copy(1, z_send.at[i, high_rows], -1),
+                held=z_waits,
             )
 
         @pl.when(is_next)
         def _():
-            start_when(is_next, lambda: z_copy(2, z_send.at[i, high_rows], 1))
+            start_when(is_next, lambda: z_copy(2, z_send.at[i, high_rows], 1), held=z_waits)
 
         @pl.when(is_back)
         def _():
-            start_when(is_back, lambda: z_copy(4, z_send.at[i, low_rows], -1))
+            start_when(is_back, lambda: z_copy(4, z_send.at[i, low_rows], -1), held=z_waits)
 
     def z_second(i):
         e = (order[i] // 2 - zh) % 4
@@ -495,13 +503,13 @@
         def _():
             z_copy(0, z_mer.at[0], 1).wait_recv()
             z_mer[0] = z_send[i, :HALF_ROWS] + z_rec[0]
-            start_when(is_next, lambda: z_copy(3, z_mer.at[0], 1))
+            start_when(is_next, lambda: z_copy(3, z_mer.at[0], 1), held=z_waits)
 
         @pl.when(is_back)
         def _():
             z_copy(1, z_mer.at[1], -1).wait_recv()
             z_mer[1] = z_send[i, HALF_ROWS:] + z_rec[1]
-            start_when(is_back, lambda: z_copy(5, z_mer.at[1], -1))
+            start_when(is_back, lambda: z_copy(5, z_mer.at[1], -1), held=z_waits)
 
     weight_grad(0)
     arrived("a", 0, 2)
@@ -552,7 +560,6 @@
     x_second(1)
     x_last(0)
     x_first(5)
-    x_first(6)
     accumulate(lambda j: order[4] * j + order[1] * (1 - j), False)
     for n in (0, 1):
         ag["za", n, 2].wait_recv()
@@ -561,6 +568,8 @@
     x_second(4)
     x_last(2)
     x_first(7)
+    x_second(5)
+    x_first(6)
     for copy in gain_x:
         copy.wait_recv()
     gain2[...] = gain1[...] + gain1_rec[0] + gain1_rec[1] + gain1_rec[2]
@@ -568,7 +577,6 @@
     x_last(1)
     accumulate(lambda j: order[6] * j + order[5] * (1 - j), False)
     x_last(3)
-    x_second(5)
     last = order[7]
     grad = jnp.concatenate([all_a[last], all_b[last]], axis=1)
     ga[...] = (gacc[...] + dot(grad, w[w_rows(last), :], 1, 0)).astype(BF16)
@@ -589,11 +597,11 @@
         gk[:, cols] = dot(gs, q[:, cols], 0, 0).astype(BF16)
         return carry
 
-    lax.fori_loop(0, 2, backward, 0)
+    lax.fori_loop(0, 1, backward, 0)
+    x_last(5)
+    lax.fori_loop(1, 3, backward, 0)
     z_second(2)
     z_second(1)
-    x_last(5)
-    lax.fori_loop(2, 3, backward, 0)
     x_last(6)
     x_last(7)
     lax.fori_loop(3, HEADS, backward, 0)
@@ -601,6 +609,10 @@
         copy.wait_recv()
     gain = gain2[...] + gain2_rec[0] + gain2_rec[1] + gain2_rec[2]
     gg_ref[...] = jnp.sum(gain, axis=0)
+    for copy in messages:
+        copy.wait_send()
+    for condition, make in waits:
+        wait_when(condition, make)
     z_second(3)
     z_second(4)
     z_second(5)
@@ -612,14 +624,8 @@
     gw_out[:HALF_ROWS] = z_own[:HALF_ROWS] + z_rec[3].astype(F32) + z_rec[4].astype(F32)
     gw_out[HALF_ROWS:] = z_own[HALF_ROWS:] + z_rec[2].astype(F32) + z_rec[5].astype(F32)
 
-    for copy in messages:
-        copy.wait_send()
-    for condition, make in waits:
-
-        @pl.when(condition)
-        def _():
-            make().wait_send()
-
+    for condition, make in z_waits:
+        wait_when(condition, make)
     assert len(messages) <= MESSAGES
 
 

time: 107 us -> 106 us (level)
  no operation moved by 1% of the time
where the time goes in v4:
time: 106 us
  Pallas kernels  103 us (97%)
  local copies, waits for them, and re-layouts  1.36 us (1%)
    pallas_call x1, Pallas kernels, shards(): pl.pallas_call(kernel, out_shape=(rows, rows, rows, rows, rows, jax.Shape...  102 us

profile of v4, /device:TPU:56, one launch (start us, length us, event | category | flops | bytes accessed | tf_op | source)
XLA Modules:
  0.0 105.6 jit_solution(6766922592545872309)
XLA Ops:
  0.6 0.0 copy-start
  0.6 0.7 copy-done
  1.3 0.0 copy-start.1
  1.3 0.7 copy-done.1
  2.0 101.8 %shard_map.144 = (bf16[384,640]{1,0:T(8,128)(2,1)S(1)}, bf16[384,640]{1,0:T(8,128)(2,1)S(1)}, bf16[384,640]{1,0:T(8,128)(2,1)S(1)}, bf16[384,640]{1,0:T(8,128)(2...) custom-call(bf16[384,640]{1,0:T(8,128)(2,1)} %q_hbm.1, bf16[384,640]{1,0:T(8,128)(2,1)} %k_hbm.1, ...), custom_call_target="tpu_custom_call" | custom-call | tf_op jit(solution)/shard_map/pallas_call | solution.py:681
  103.8 1.6 %shard_map.145 = (bf16[384,640]{1,0:T(8,128)(2,1)}, bf16[384,640]{1,0:T(8,128)(2,1)}, bf16[384,640]{1,0:T(8,128)(2,1)}, bf16[384,640]{1,0:T(8,128)(2,1)}, bf16[3...) custom-call(bf16[384,640]{1,0:T(8,128)(2,1)S(1)} %get-tuple-element.14.refs_0_, ...), custom_call_target="tpu_custom_call" | custom-call | tf_op jit(solution)/shard_map/pallas_call | solution.py:644
Async XLA Ops:
  0.6 0.7 copy-start
  1.3 0.7 copy-start.1

commit v5 on v4

--- a/solution.py
+++ b/solution.py
@@ -602,8 +602,11 @@
     lax.fori_loop(1, 3, backward, 0)
     z_second(2)
     z_second(1)
+    x_last(7)
     x_last(6)
-    x_last(7)
+    z_second(3)
+    z_second(4)
+    z_second(5)
     lax.fori_loop(3, HEADS, backward, 0)
     for copy in gain_z:
         copy.wait_recv()
@@ -613,11 +616,8 @@
         copy.wait_send()
     for condition, make in waits:
         wait_when(condition, make)
-    z_second(3)
-    z_second(4)
-    z_second(5)
+    z_second(7)
     z_second(6)
-    z_second(7)
 
     for kind in (2, 3, 4, 5):
         z_copy(kind, z_mer.at[0], 1).wait_recv()

time: 106 us -> 106 us (level)
  no operation moved by 1% of the time
where the time goes in v5:
time: 106 us
  Pallas kernels  104 us (98%)
  local copies, waits for them, and re-layouts  1.36 us (1%)
    pallas_call x1, Pallas kernels, shards(): pl.pallas_call(kernel, out_shape=(rows, rows, rows, rows, rows, jax.Shape...  102 us

profile of v5, /device:TPU:56, one launch (start us, length us, event | category | flops | bytes accessed | tf_op | source)
XLA Modules:
  0.0 105.7 jit_solution(16134359440073881393)
XLA Ops:
  0.6 0.0 copy-start
  0.6 0.7 copy-done
  1.3 0.0 copy-start.1
  1.3 0.7 copy-done.1
  2.0 101.9 %shard_map.144 = (bf16[384,640]{1,0:T(8,128)(2,1)S(1)}, bf16[384,640]{1,0:T(8,128)(2,1)S(1)}, bf16[384,640]{1,0:T(8,128)(2,1)S(1)}, bf16[384,640]{1,0:T(8,128)(2...) custom-call(bf16[384,640]{1,0:T(8,128)(2,1)} %q_hbm.1, bf16[384,640]{1,0:T(8,128)(2,1)} %k_hbm.1, ...), custom_call_target="tpu_custom_call" | custom-call | tf_op jit(solution)/shard_map/pallas_call | solution.py:681
  103.9 1.6 %shard_map.145 = (bf16[384,640]{1,0:T(8,128)(2,1)}, bf16[384,640]{1,0:T(8,128)(2,1)}, bf16[384,640]{1,0:T(8,128)(2,1)}, bf16[384,640]{1,0:T(8,128)(2,1)}, bf16[3...) custom-call(bf16[384,640]{1,0:T(8,128)(2,1)S(1)} %get-tuple-element.14.refs_0_, ...), custom_call_target="tpu_custom_call" | custom-call | tf_op jit(solution)/shard_map/pallas_call | solution.py:644
Async XLA Ops:
  0.6 0.7 copy-start
  1.3 0.7 copy-start.1
